TPU v7x, 32 devices: a whole 2x2x4 slice. The times are simulated.
32 devices in a mesh: inner: 4 (over z), outer: 8 (over y, x, core).
Axes of the slice: x: 2, y: 2, z: 4, core: 2. Of those that a mesh axis runs over, the one named last changes fastest.
Arguments:
- inner_state: float32 [2, 16, 2048], P(None, 'inner', 'outer'), may hold values from -6 to 6
- outer_state: float32 [2, 640, 4096], P(None, 'inner', 'outer'), may hold values from -6 to 6
- energies: float32 [16, 2048], P('inner', 'outer'), may hold values from -2 to 2
- dipole: float32 [16, 2048, 2048], P('inner', 'outer'), may hold values from -0.125 to 0.125
- surface: float32 [16, 40, 2048], P('inner', None, 'outer'), may hold values from -0.125 to 0.125
- thresholds: float32 [640], P('inner'), may hold values from 0 to 2
- coupling_coef: float32 [16, 40, 40], P('inner'), may hold values from -1 to 1
- coupling_pattern: int32 [16, 40, 40], P('inner'), may hold values 0 or 1
- block_sizes: int32 [16], P('inner'), may hold values from 1 to 2048, 30720 in all
- field_strength: float32 [2], replicated, may hold values from 0.5 to 2
Outputs:
- inner_final: float32 [2, 16, 2048], P(None, 'inner', 'outer')
- outer_final: float32 [2, 640, 4096], P(None, 'inner', 'outer')
All inputs are finite; a program needn't handle non-finite values. No bound on the sum of `coupling_pattern` or of `block_sizes` on one device may be relied on, other than what follows from the above.
Results may differ from a plain program's by a relative error of at most 0.0001.
Values sent between devices are 32-bit elements; how exact they have to be, the bound alone decides.
A program may use at most 128 MiB of HBM per device.

v0:
```python
import jax
import jax.numpy as jnp
from jax import lax
from jax.sharding import PartitionSpec as P

STEPS = 2
ORDER = 4
kinetic_scale = 3.125
time_step = 0.1


def from_behind(block, axis, distance):
    devices = range(lax.axis_size(axis))
    route = [(i - distance, i) for i in devices if i - distance in devices]
    return lax.ppermute(block, axis, route)


def spread(shard, axis, root):
    mine = lax.axis_index(axis) == root
    return lax.psum(jnp.where(mine, shard, jnp.zeros_like(shard)), axis)


def with_halo(cells, sides, width):
    for axis, dim in sides:
        count = lax.axis_size(axis)
        ends = count - 1
        head = lax.slice_in_dim(cells, 0, width, axis=dim)
        tail = lax.slice_in_dim(cells, cells.shape[dim] - width, cells.shape[dim], axis=dim)
        cells = jnp.concatenate(
            [
                lax.ppermute(tail, axis, [(i, (i + 1) % count) for i in range(ends)]),
                cells,
                lax.ppermute(head, axis, [((i + 1) % count, i) for i in range(ends)]),
            ],
            axis=dim,
        )
    return cells


def reduce_partials(partial_terms, partial_boundary):
    own_terms = lax.psum_scatter(partial_terms, "outer", scatter_dimension=2, tiled=True)
    boundary = lax.psum(partial_boundary, "outer")
    return (own_terms, boundary)


def local(
    inner_state,
    outer_state,
    energies,
    dipole,
    surface,
    thresholds,
    coupling_coef,
    coupling_pattern,
    block_sizes,
    field_strength,
):
    highest = lax.Precision.HIGHEST
    blocks = dipole.shape[0]
    row_count = dipole.shape[1]
    channels = coupling_coef.shape[1]
    radial = outer_state.shape[2]
    sector_index = lax.axis_index("outer")
    row_index = sector_index * row_count + jnp.arange(row_count, dtype=jnp.int32)
    live_rows = (row_index[None, :] < block_sizes[:, None]).astype(jnp.float32)
    coupling = coupling_coef * coupling_pattern.astype(jnp.float32)
    first_sector = jnp.where(sector_index == 0, 1.0, 0.0).astype(jnp.float32)
    edge_mask = first_sector * (jnp.arange(radial, dtype=jnp.int32) == 0).astype(jnp.float32)
    prev_dipole, prev_coupling = from_behind((dipole[blocks - 1], coupling[blocks - 1]), "inner", 1)
    current = (inner_state * live_rows, outer_state)
    for time_index in range(STEPS):
        strength = field_strength[time_index]
        taylor_term = current
        accumulated = current
        for power in range(1, ORDER + 1):
            inner_part = taylor_term[0]
            outer_part = taylor_term[1]
            channel_grid = outer_part.reshape(2, blocks, channels, radial)
            next_first, next_channels = from_behind(
                (inner_part[:, 0], channel_grid[:, 0]), "inner", -1
            )
            extended = jnp.concatenate([inner_part, next_first[:, None]], axis=1)
            gathered = lax.all_gather(extended, "outer", axis=2, tiled=True)
            edge_values = spread(outer_part[:, :, 0], "outer", 0)
            forward = jnp.einsum("lij,plj->pli", dipole, gathered[:, 1:], precision=highest)
            grid_next = jnp.concatenate([channel_grid[:, 1:], next_channels[:, None]], axis=1)
            upward = jnp.einsum("lab,plbr->plar", coupling, grid_next, precision=highest)
            partial_boundary = jnp.einsum("lcs,pls->plc", surface, inner_part, precision=highest)
            prev_rows, prev_channels = from_behind(
                (inner_part[:, blocks - 1], channel_grid[:, blocks - 1]), "inner", 1
            )
            source_rows = jnp.concatenate([prev_rows[:, None], inner_part[:, : blocks - 1]], axis=1)
            source_blocks = jnp.concatenate([prev_dipole[None], dipole[: blocks - 1]], axis=0)
            partial_terms = jnp.einsum(
                "lji,plj->pli", source_blocks, source_rows, precision=highest
            )
            backward, boundary = reduce_partials(partial_terms, partial_boundary)
            source_grid = jnp.concatenate(
                [prev_channels[:, None], channel_grid[:, : blocks - 1]], axis=1
            )
            source_coupling = jnp.concatenate([prev_coupling[None], coupling[: blocks - 1]], axis=0)
            downward = jnp.einsum("lba,plbr->plar", source_coupling, source_grid, precision=highest)
            first_point = edge_values.reshape(2, blocks, channels)
            surf_term = jnp.einsum("lcs,plc->pls", surface, first_point, precision=highest)
            inner_image = live_rows * (
                energies * inner_part + strength * (forward + backward) - kinetic_scale * surf_term
            )
            padded = with_halo(outer_part, (("outer", 2),), 1)
            left_cells = (
                padded[:, :, :radial]
                + edge_mask[None, None, :] * boundary.reshape(2, blocks * channels)[:, :, None]
            )
            right_cells = padded[:, :, 2:]
            kinetic = kinetic_scale * (2.0 * outer_part - left_cells - right_cells)
            outer_image = (
                kinetic
                + thresholds[None, :, None] * outer_part
                + strength * (upward + downward).reshape(2, blocks * channels, radial)
            )
            inner_image, outer_image = (inner_image, outer_image)
            factor = time_step / power
            taylor_term = (
                factor * jnp.stack([inner_image[1], -inner_image[0]]),
                factor * jnp.stack([outer_image[1], -outer_image[0]]),
            )
            accumulated = (accumulated[0] + taylor_term[0], accumulated[1] + taylor_term[1])
        current = accumulated
    return (current[0], current[1])


def solution(mesh):
    placed = (
        P(None, "inner", "outer"),
        P(None, "inner", "outer"),
        P("inner", "outer"),
        P("inner", "outer", None),
        P("inner", None, "outer"),
        P("inner"),
        P("inner", None, None),
        P("inner", None, None),
        P("inner"),
        P(),
    )
    return jax.shard_map(
        local,
        mesh=mesh,
        in_specs=placed,
        out_specs=(P(None, "inner", "outer"), P(None, "inner", "outer")),
        check_vma=False,
    )
```

profile of v0, /device:TPU:12, one launch (start us, length us, event | category | flops | bytes accessed | tf_op | source)
XLA Modules:
  0.0 834.8 jit_solution(18084127534141652575)
XLA Ops:
  8.7 3.5 collective-permute-start.1
  15.4 3.5 collective-permute-start.2
  34.9 12.6 %all-reduce.7 = (f32[2,160]{1,0:T(2,128)}, f32[2,4,40]{2,0,1:T(2,128)S(1)}) all-reduce(f32[2,160]{1,0:T(2,128)S(1)} %mul.616, f32[2,4,40]{2,0,1:T(2,128)S(1)} %copy.69), channel_id=1, replica_groups=mesh['inner'=4,'outer'=8] {'outer'}, use_global_device_ids=true, to_apply=%region_3.4 | all-reduce | flops 640 | bytes 5120 | tf_op jit(solution)/shard_map/psum | solution.py:42
  48.9 6.3 slice.446
  55.2 4.7 collective-permute-start.7
  59.9 8.3 all_gather.24
  70.5 4.2 collective-permute-start.6
  84.6 3.9 collective-permute-start.14
  91.3 4.5 collective-permute-start.13
  97.4 7.4 convolution_bitcast_fusion.7
  104.9 4.2 copy.137
  109.1 4.5 reshape.173
  117.4 30.5 %reduce-scatter.25.cloned.1.call-done = f32[256,8]{1,0:T(8,128)} async-done(((f32[2048,8]{1,0:T(8,128)}), f32[256,8]{1,0:T(8,128)}) %reduce-scatter.25.cloned.1.call-update) | async-done | bytes 8208
  151.2 9.8 %fusion.55 = f32[2,4,256]{2,0,1:T(2,128)S(1)} fusion(f32[2,4,256]{2,0,1:T(2,128)S(1)} %fusion.63, f32[2,4,256]{2,0,1:T(2,128)S(1)} %copy.138, f32[2,5,2048]{2,0,1:T(2,128)S(1)} %all_gather.24, f32[4,256,2048]{2,1,0:T(8,128)} %param.13, f32[2,4,256]{2,0,1:T(2,128)S(1)} %copy-done.49, f32[]{:T(128)} %bitcast, f32[4,256]{1,0:T(4,128)S(1)} %copy-done.53, ...), kind=kOutput, calls=%fused_computation.81 | convolution fusion | flops 50343936 | bytes 8511492 | tf_op jit(solution)/shard_map/lij,plj->pli/dot_general | solution.py:85
  161.4 12.6 %all-reduce.6 = (f32[2,160]{1,0:T(2,128)S(1)}, f32[2,4,40]{2,0,1:T(2,128)S(1)}) all-reduce(f32[2,160]{1,0:T(2,128)S(1)} %mul.639, f32[2,4,40]{2,0,1:T(2,128)S(1)} %copy.79), channel_id=1, replica_groups=mesh['inner'=4,'outer'=8] {'outer'}, use_global_device_ids=true, to_apply=%region_6.7 | all-reduce | flops 640 | bytes 5120 | tf_op jit(solution)/shard_map/psum | solution.py:42
  194.4 4.5 collective-permute-start.19
  199.0 6.8 convolution_bitcast_fusion.6
  209.0 4.5 reshape.175
  213.6 7.7 all_gather.25
  221.3 28.3 %reduce-scatter.27.cloned.1.call-done = f32[256,8]{1,0:T(8,128)} async-done(((f32[2048,8]{1,0:T(8,128)}), f32[256,8]{1,0:T(8,128)}) %reduce-scatter.27.cloned.1.call-update) | async-done | bytes 8208
  252.8 9.8 %fusion.50 = f32[2,4,256]{2,0,1:T(2,128)S(1)} fusion(f32[2,4,256]{2,0,1:T(2,128)S(1)} %fusion.62, f32[2,4,256]{2,0,1:T(2,128)S(1)} %copy.140, f32[2,5,2048]{2,0,1:T(2,128)S(1)} %all_gather.25, f32[4,256,2048]{2,1,0:T(8,128)} %param.13, f32[4,256]{1,0:T(4,128)S(1)} %get-tuple-element.129, f32[]{:T(128)} %bitcast, f32[4,256]{1,0:T(4,128)S(1)} %compare_convert_fusion, ...), kind=kOutput, calls=%fused_computation.75 | convolution fusion | flops 50345984 | bytes 8511492 | tf_op jit(solution)/shard_map/lij,plj->pli/dot_general | solution.py:85
  266.4 12.8 %all-reduce.5 = (f32[2,160]{1,0:T(2,128)}, f32[2,4,40]{2,0,1:T(2,128)S(1)}) all-reduce(f32[2,160]{1,0:T(2,128)S(1)} %mul.662, f32[2,4,40]{2,0,1:T(2,128)S(1)} %copy.83), channel_id=1, replica_groups=mesh['inner'=4,'outer'=8] {'outer'}, use_global_device_ids=true, to_apply=%region_9.10 | all-reduce | flops 640 | bytes 5120 | tf_op jit(solution)/shard_map/psum | solution.py:42
  282.0 6.8 convolution_bitcast_fusion.5
  292.0 4.5 reshape.177
  296.6 8.4 %all_gather.26 = f32[2,5,2048]{2,0,1:T(2,128)S(1)} all-gather(f32[2,5,256]{2,0,1:T(2,128)S(1)} %pad_maximum_fusion.25), channel_id=1, replica_groups=mesh['inner'=4,'outer'=8] {'outer'}, dimensions={2}, use_global_device_ids=true | all-gather | bytes 92160 | tf_op jit(solution)/shard_map/all_gather | solution.py:83
  315.8 3.4 collective-permute-start.27
  324.2 4.5 collective-permute-start.25
  328.8 4.2 reduce-scatter.29.cloned.1.call-done
  336.2 9.8 %fusion.45 = f32[2,4,256]{2,0,1:T(2,128)S(1)} fusion(f32[2,4,256]{2,0,1:T(2,128)S(1)} %fusion.61, f32[2,4,256]{2,0,1:T(2,128)S(1)} %copy.142, f32[2,5,2048]{2,0,1:T(2,128)S(1)} %all_gather.26, f32[4,256,2048]{2,1,0:T(8,128)} %param.13, f32[4,256]{1,0:T(4,128)S(1)} %get-tuple-element.130, f32[]{:T(128)} %bitcast, f32[4,256]{1,0:T(4,128)S(1)} %compare_convert_fusion, ...), kind=kOutput, calls=%fused_computation.69 | convolution fusion | flops 50345984 | bytes 8511492 | tf_op jit(solution)/shard_map/lij,plj->pli/dot_general | solution.py:85
  346.3 3.7 collective-permute-start.17
  350.1 12.7 %all-reduce.4 = (f32[2,160]{1,0:T(2,128)}, f32[2,4,40]{2,0,1:T(2,128)S(1)}) all-reduce(f32[2,160]{1,0:T(2,128)S(1)} %mul.684, f32[2,4,40]{2,0,1:T(2,128)} %copy.87), channel_id=1, replica_groups=mesh['inner'=4,'outer'=8] {'outer'}, use_global_device_ids=true, to_apply=%region_12.13 | all-reduce | flops 640 | bytes 5120 | tf_op jit(solution)/shard_map/psum | solution.py:42
  365.9 6.8 convolution_bitcast_fusion.4
  375.9 4.5 reshape.179
  380.6 8.0 all_gather.27
  388.6 28.1 %reduce-scatter.31.cloned.1.call-done = f32[256,8]{1,0:T(8,128)} async-done(((f32[2048,8]{1,0:T(8,128)}), f32[256,8]{1,0:T(8,128)}) %reduce-scatter.31.cloned.1.call-update) | async-done | bytes 8208
  419.8 9.8 %fusion.40 = f32[2,4,256]{2,0,1:T(2,128)S(1)} fusion(f32[2,4,256]{2,0,1:T(2,128)} %fusion.60, f32[2,4,256]{2,0,1:T(2,128)S(1)} %copy.144, f32[2,5,2048]{2,0,1:T(2,128)S(1)} %all_gather.27, f32[4,256,2048]{2,1,0:T(8,128)} %param.13, f32[4,256]{1,0:T(4,128)S(1)} %get-tuple-element.128, f32[]{:T(128)} %bitcast, f32[4,256]{1,0:T(4,128)S(1)} %compare_convert_fusion, ...), kind=kOutput, calls=%fused_computation.63 | convolution fusion | flops 50345984 | bytes 8511492 | tf_op jit(solution)/shard_map/lij,plj->pli/dot_general | solution.py:85
  438.0 6.8 convolution_bitcast_fusion.3
  448.6 4.5 reshape.181
  453.2 8.3 all_gather.28
  472.7 14.2 %all-reduce.3 = (f32[2,160]{1,0:T(2,128)}, f32[2,4,40]{2,0,1:T(2,128)}) all-reduce(f32[2,160]{1,0:T(2,128)} %mul.704, f32[2,4,40]{2,0,1:T(2,128)S(1)} %copy.91), channel_id=1, replica_groups=mesh['inner'=4,'outer'=8] {'outer'}, use_global_device_ids=true, to_apply=%region_15.16 | all-reduce | flops 640 | bytes 5120 | tf_op jit(solution)/shard_map/psum | solution.py:42
  488.4 3.8 collective-permute-start.33
  496.8 4.9 collective-permute-start.31
  505.6 9.8 %fusion.35 = f32[2,4,256]{2,0,1:T(2,128)S(1)} fusion(f32[2,4,256]{2,0,1:T(2,128)} %fusion.59, f32[2,4,256]{2,0,1:T(2,128)} %copy.146, f32[2,5,2048]{2,0,1:T(2,128)S(1)} %all_gather.28, f32[4,256,2048]{2,1,0:T(8,128)} %param.13, f32[2,4,256]{2,0,1:T(2,128)S(1)} %fusion.196, f32[]{:T(128)} %bitcast.65, f32[4,256]{1,0:T(4,128)S(1)} %copy-done.53, ...), kind=kOutput, calls=%fused_computation.57 | convolution fusion | flops 50343936 | bytes 8511492 | tf_op jit(solution)/shard_map/lij,plj->pli/dot_general | solution.py:85
  523.5 6.8 convolution_bitcast_fusion.2
  533.5 4.5 reshape.183
  538.8 7.5 all_gather.29
  557.7 14.5 %all-reduce.2 = (f32[2,160]{1,0:T(2,128)}, f32[2,4,40]{2,0,1:T(2,128)}) all-reduce(f32[2,160]{1,0:T(2,128)} %mul.721, f32[2,4,40]{2,0,1:T(2,128)S(1)} %copy.99), channel_id=1, replica_groups=mesh['inner'=4,'outer'=8] {'outer'}, use_global_device_ids=true, to_apply=%region_18.19 | all-reduce | flops 640 | bytes 5120 | tf_op jit(solution)/shard_map/psum | solution.py:42
  573.7 3.9 collective-permute-start.39
  582.1 4.5 collective-permute-start.37
  590.5 9.8 %fusion.30 = f32[2,4,256]{2,0,1:T(2,128)S(1)} fusion(f32[2,4,256]{2,0,1:T(2,128)} %fusion.58, f32[2,4,256]{2,0,1:T(2,128)} %copy.148, f32[2,5,2048]{2,0,1:T(2,128)S(1)} %all_gather.29, f32[4,256,2048]{2,1,0:T(8,128)} %param.13, f32[]{:T(128)} %bitcast.65, f32[4,256]{1,0:T(4,128)S(1)} %copy-done.55, f32[4,256]{1,0:T(4,128)S(1)} %compare_convert_fusion, ...), kind=kOutput, calls=%fused_computation.51 | convolution fusion | flops 50345984 | bytes 8511492 | tf_op jit(solution)/shard_map/lij,plj->pli/dot_general | solution.py:85
  608.4 6.8 convolution_bitcast_fusion.1
  618.4 4.5 reshape.185
  623.7 7.7 all_gather.30
  631.3 28.7 %reduce-scatter.37.cloned.1.call-done = f32[256,8]{1,0:T(8,128)} async-done(((f32[2048,8]{1,0:T(8,128)}), f32[256,8]{1,0:T(8,128)}) %reduce-scatter.37.cloned.1.call-update) | async-done | bytes 8208
  677.2 13.2 %all-reduce.1 = (f32[2,160]{1,0:T(2,128)}, f32[2,4,40]{2,0,1:T(2,128)}) all-reduce(f32[2,160]{1,0:T(2,128)} %mul.738, f32[2,4,40]{2,0,1:T(2,128)} %copy.103), channel_id=1, replica_groups=mesh['inner'=4,'outer'=8] {'outer'}, use_global_device_ids=true, to_apply=%region_21.22 | all-reduce | flops 640 | bytes 5120 | tf_op jit(solution)/shard_map/psum | solution.py:42
  691.3 9.8 %fusion.25 = f32[2,4,256]{2,0,1:T(2,128)S(1)} fusion(f32[2,4,256]{2,0,1:T(2,128)S(1)} %fusion.57, f32[2,4,256]{2,0,1:T(2,128)} %copy.150, f32[2,5,2048]{2,0,1:T(2,128)S(1)} %all_gather.30, f32[4,256,2048]{2,1,0:T(8,128)} %param.13, f32[]{:T(128)} %bitcast.65, f32[4,256]{1,0:T(4,128)S(1)} %get-tuple-element.130, f32[4,256]{1,0:T(4,128)S(1)} %compare_convert_fusion, ...), kind=kOutput, calls=%fused_computation.45 | convolution fusion | flops 50345984 | bytes 8511492 | tf_op jit(solution)/shard_map/lij,plj->pli/dot_general | solution.py:85
  714.4 4.5 collective-permute-start.43
  721.3 6.8 convolution_bitcast_fusion
  731.3 4.6 reshape.187
  736.6 7.5 all_gather.31
  744.0 28.4 %reduce-scatter.39.cloned.1.call-done = f32[256,8]{1,0:T(8,128)} async-done(((f32[2048,8]{1,0:T(8,128)}), f32[256,8]{1,0:T(8,128)}) %reduce-scatter.39.cloned.1.call-update) | async-done | bytes 8208
  791.1 4.5 collective-permute-start.47
  795.6 13.1 %all-reduce = (f32[2,4,40]{2,0,1:T(2,128)S(1)}, f32[2,160]{1,0:T(2,128)S(1)}) all-reduce(f32[2,4,40]{2,0,1:T(2,128)S(1)} %copy.107, f32[2,160]{1,0:T(2,128)S(1)} %mul.753), channel_id=1, replica_groups=mesh['inner'=4,'outer'=8] {'outer'}, use_global_device_ids=true, to_apply=%region_22.23 | all-reduce | flops 640 | bytes 5120 | tf_op jit(solution)/shard_map/psum | solution.py:20
  809.1 10.4 %fusion.20 = f32[2,4,256]{2,0,1:T(2,128)S(1)} fusion(f32[2,4,256]{2,0,1:T(2,128)S(1)} %fusion.56, f32[2,4,256]{2,0,1:T(2,128)S(1)} %copy.152, f32[2,5,2048]{2,0,1:T(2,128)S(1)} %all_gather.31, f32[4,256,2048]{2,1,0:T(8,128)} %param.13, f32[]{:T(128)} %bitcast.65, f32[4,256]{1,0:T(4,128)S(1)} %get-tuple-element.128, f32[4,256]{1,0:T(4,128)S(1)} %compare_convert_fusion, ...), kind=kOutput, calls=%fused_computation.39 | convolution fusion | flops 50345984 | bytes 8511492 | tf_op jit(solution)/shard_map/lij,plj->pli/dot_general | solution.py:85
  (452 shorter events, 252.7 us)
Async XLA Ops:
  7.2 140.7 %reduce-scatter.25.cloned.1.call-start = ((), (), s32[]{:S(2)}) async-start(), calls=%async_computation.8 | async-start | bytes 1179648
  8.7 51.2 %copy-start.48 = (f32[2,4,256]{2,0,1:T(2,128)}, f32[2,4,256]{2,0,1:T(2,128)S(1)}, u32[]{:S(2)}) copy-start(f32[2,4,256]{2,0,1:T(2,128)S(1)} %copy_multiply_fusion) | copy-start | bytes 24580
  8.7 88.7 %collective-permute-start.1 = (f32[2,256]{1,0:T(2,128)S(1)}, f32[2,256]{1,0:T(2,128)S(1)}, u32[]{:S(2)}, u32[]{:S(2)}) collective-permute-start(f32[2,256]{1,0:T(2,128)S(1)} %get-tuple-element.127), channel_id=1, source_target_pairs={{0,8},{8,16},{16,24},{1,9},{9,17},{17,25},{2,10},{10,18},{18,26},{... | collective-permute-start | bytes 6152 | tf_op jit(solution)/shard_map/ppermute | solution.py:15
  15.4 82.0 %collective-permute-start.2 = (f32[256,2048]{1,0:T(8,128)}, f32[256,2048]{1,0:T(8,128)S(1)}, u32[]{:S(2)}, u32[]{:S(2)}) collective-permute-start(f32[256,2048]{1,0:T(8,128)} %slice_bitcast_fusion), channel_id=1, source_target_pairs={{0,8},{8,16},{16,24},{1,9},{9,17},{17,25},{2,10},{10,18},{18,26},{... | collective-permute-start | bytes 6291464 | tf_op jit(solution)/shard_map/ppermute | solution.py:15
  18.9 36.3 %collective-permute-start = (f32[2,256]{1,0:T(2,128)S(1)}, f32[2,256]{1,0:T(2,128)S(1)}, u32[]{:S(2)}, u32[]{:S(2)}) collective-permute-start(f32[2,256]{1,0:T(2,128)S(1)} %get-tuple-element.126), channel_id=1, source_target_pairs={{8,0},{16,8},{24,16},{9,1},{17,9},{25,17},{10,2},{18,10},{26,18},{... | collective-permute-start | bytes 6152 | tf_op jit(solution)/shard_map/ppermute | solution.py:15
  24.0 44.3 %collective-permute-start.9 = (f32[40,40]{0,1:T(8,128)}, f32[40,40]{0,1:T(8,128)S(1)}, u32[]{:S(2)}, u32[]{:S(2)}) collective-permute-start(f32[40,40]{0,1:T(8,128)} %slice_bitcast_fusion.17), channel_id=1, source_target_pairs={{0,8},{8,16},{16,24},{1,9},{9,17},{17,25},{2,10},{10,18},{18,26},{... | collective-permute-start | bytes 19208 | tf_op jit(solution)/shard_map/ppermute | solution.py:15
  28.4 42.2 %collective-permute-start.8 = (f32[2,40,512]{2,1,0:T(8,128)S(1)}, f32[2,40,512]{2,1,0:T(8,128)}, u32[]{:S(2)}, u32[]{:S(2)}) collective-permute-start(f32[2,40,512]{2,1,0:T(8,128)S(1)} %get-tuple-element.95), channel_id=1, source_target_pairs={{0,8},{8,16},{16,24},{1,9},{9,17},{17,25},{2,10},{10,18},{18,26},{... | collective-permute-start | bytes 491528 | tf_op jit(solution)/shard_map/ppermute | solution.py:15
  48.2 204.6 %copy-start.54 = (f32[4,256]{1,0:T(4,128)}, f32[4,256]{1,0:T(4,128)S(1)}, u32[]{:S(2)}) copy-start(f32[4,256]{1,0:T(4,128)S(1)} %get-tuple-element.129) | copy-start | bytes 12292
  55.2 21.2 %collective-permute-start.7 = (f32[2,40,512]{2,1,0:T(8,128)S(1)}, f32[2,40,512]{2,1,0:T(8,128)S(1)}, u32[]{:S(2)}, u32[]{:S(2)}) collective-permute-start(f32[2,40,512]{2,1,0:T(8,128)S(1)} %get-tuple-element.94), channel_id=1, source_target_pairs={{8,0},{16,8},{24,16},{9,1},{17,9},{25,17},{10,2},{18,10},{26,18},{... | collective-permute-start | bytes 491528 | tf_op jit(solution)/shard_map/ppermute | solution.py:15
  68.3 9.5 %collective-permute-start.5 = (f32[2,160,1]{2,1,0:T(8,128)S(1)}, f32[2,160,1]{2,1,0:T(8,128)S(1)}, u32[]{:S(2)}, u32[]{:S(2)}) collective-permute-start(f32[2,160,1]{2,1,0:T(8,128)S(1)} %copy-done.51), channel_id=1, source_target_pairs={{0,1},{1,2},{2,3},{3,4},{4,5},{5,6},{6,7},{8,9},{9,10},{10,11},{11... | collective-permute-start | bytes 3848 | tf_op jit(solution)/shard_map/ppermute | solution.py:31
  70.5 7.2 collective-permute-start.6
  82.6 8.7 %collective-permute-start.15 = (f32[2,40,512]{2,1,0:T(8,128)S(1)}, f32[2,40,512]{2,1,0:T(8,128)S(1)}, u32[]{:S(2)}, u32[]{:S(2)}) collective-permute-start(f32[2,40,512]{2,1,0:T(8,128)S(1)} %get-tuple-element.86), channel_id=1, source_target_pairs={{0,8},{8,16},{16,24},{1,9},{9,17},{17,25},{2,10},{10,18},{18,26},{... | collective-permute-start | bytes 491528 | tf_op jit(solution)/shard_map/ppermute | solution.py:15
  84.6 29.3 %collective-permute-start.14 = (f32[2,40,512]{2,1,0:T(8,128)}, f32[2,40,512]{2,1,0:T(8,128)}, u32[]{:S(2)}, u32[]{:S(2)}) collective-permute-start(f32[2,40,512]{2,1,0:T(8,128)} %get-tuple-element.85), channel_id=1, source_target_pairs={{8,0},{16,8},{24,16},{9,1},{17,9},{25,17},{10,2},{18,10},{26,18},{... | collective-permute-start | bytes 491528 | tf_op jit(solution)/shard_map/ppermute | solution.py:15
  88.5 85.4 %collective-permute-start.12 = (f32[2,160,1]{2,1,0:T(8,128)}, f32[2,160,1]{2,1,0:T(8,128)}, u32[]{:S(2)}, u32[]{:S(2)}) collective-permute-start(f32[2,160,1]{2,1,0:T(8,128)} %get-tuple-element.81), channel_id=1, source_target_pairs={{0,1},{1,2},{2,3},{3,4},{4,5},{5,6},{6,7},{8,9},{9,10},{10,11},{11... | collective-permute-start | bytes 3848 | tf_op jit(solution)/shard_map/ppermute | solution.py:31
  91.3 82.6 %collective-permute-start.13 = (f32[2,160,1]{2,1,0:T(8,128)}, f32[2,160,1]{2,1,0:T(8,128)}, u32[]{:S(2)}, u32[]{:S(2)}) collective-permute-start(f32[2,160,1]{2,1,0:T(8,128)} %get-tuple-element.82), channel_id=1, source_target_pairs={{1,0},{2,1},{3,2},{4,3},{5,4},{6,5},{7,6},{9,8},{10,9},{11,10},{12... | collective-permute-start | bytes 3848 | tf_op jit(solution)/shard_map/ppermute | solution.py:33
  113.7 135.9 %reduce-scatter.27.cloned.1.call-start = ((), (), s32[]{:S(2)}) async-start(), calls=%async_computation.9 | async-start | bytes 1179648
  179.0 15.4 %collective-permute-start.4 = (f32[2,256]{1,0:T(2,128)S(1)}, f32[2,256]{1,0:T(2,128)S(1)}, u32[]{:S(2)}, u32[]{:S(2)}) collective-permute-start(f32[2,256]{1,0:T(2,128)S(1)} %get-tuple-element.123), channel_id=1, source_target_pairs={{0,8},{8,16},{16,24},{1,9},{9,17},{17,25},{2,10},{10,18},{18,26},{... | collective-permute-start | bytes 6152 | tf_op jit(solution)/shard_map/ppermute | solution.py:15
  182.4 31.2 %collective-permute-start.3 = (f32[2,256]{1,0:T(2,128)S(1)}, f32[2,256]{1,0:T(2,128)S(1)}, u32[]{:S(2)}, u32[]{:S(2)}) collective-permute-start(f32[2,256]{1,0:T(2,128)S(1)} %get-tuple-element.122), channel_id=1, source_target_pairs={{8,0},{16,8},{24,16},{9,1},{17,9},{25,17},{10,2},{18,10},{26,18},{... | collective-permute-start | bytes 6152 | tf_op jit(solution)/shard_map/ppermute | solution.py:15
  186.0 119.1 %collective-permute-start.21 = (f32[2,40,512]{2,1,0:T(8,128)}, f32[2,40,512]{2,1,0:T(8,128)}, u32[]{:S(2)}, u32[]{:S(2)}) collective-permute-start(f32[2,40,512]{2,1,0:T(8,128)} %get-tuple-element.77), channel_id=1, source_target_pairs={{0,8},{8,16},{16,24},{1,9},{9,17},{17,25},{2,10},{10,18},{18,26},{... | collective-permute-start | bytes 491528 | tf_op jit(solution)/shard_map/ppermute | solution.py:15
  189.4 117.4 %collective-permute-start.20 = (f32[2,40,512]{2,1,0:T(8,128)}, f32[2,40,512]{2,1,0:T(8,128)}, u32[]{:S(2)}, u32[]{:S(2)}) collective-permute-start(f32[2,40,512]{2,1,0:T(8,128)} %get-tuple-element.76), channel_id=1, source_target_pairs={{8,0},{16,8},{24,16},{9,1},{17,9},{25,17},{10,2},{18,10},{26,18},{... | collective-permute-start | bytes 491528 | tf_op jit(solution)/shard_map/ppermute | solution.py:15
  192.5 116.8 %collective-permute-start.18 = (f32[2,160,1]{2,1,0:T(8,128)}, f32[2,160,1]{2,1,0:T(8,128)}, u32[]{:S(2)}, u32[]{:S(2)}) collective-permute-start(f32[2,160,1]{2,1,0:T(8,128)} %get-tuple-element.72), channel_id=1, source_target_pairs={{0,1},{1,2},{2,3},{3,4},{4,5},{5,6},{6,7},{8,9},{9,10},{10,11},{11... | collective-permute-start | bytes 3848 | tf_op jit(solution)/shard_map/ppermute | solution.py:31
  194.4 114.9 %collective-permute-start.19 = (f32[2,160,1]{2,1,0:T(8,128)}, f32[2,160,1]{2,1,0:T(8,128)}, u32[]{:S(2)}, u32[]{:S(2)}) collective-permute-start(f32[2,160,1]{2,1,0:T(8,128)} %get-tuple-element.73), channel_id=1, source_target_pairs={{1,0},{2,1},{3,2},{4,3},{5,4},{6,5},{7,6},{9,8},{10,9},{11,10},{12... | collective-permute-start | bytes 3848 | tf_op jit(solution)/shard_map/ppermute | solution.py:33
  213.5 119.4 %reduce-scatter.29.cloned.1.call-start = ((), (), s32[]{:S(2)}) async-start(), calls=%async_computation.10 | async-start | bytes 1179648
  263.0 16.5 %collective-permute-start.11 = (f32[2,256]{1,0:T(2,128)S(1)}, f32[2,256]{1,0:T(2,128)S(1)}, u32[]{:S(2)}, u32[]{:S(2)}) collective-permute-start(f32[2,256]{1,0:T(2,128)S(1)} %get-tuple-element.119), channel_id=1, source_target_pairs={{0,8},{8,16},{16,24},{1,9},{9,17},{17,25},{2,10},{10,18},{18,26},{... | collective-permute-start | bytes 6152 | tf_op jit(solution)/shard_map/ppermute | solution.py:15
  279.5 9.3 %collective-permute-start.10 = (f32[2,256]{1,0:T(2,128)S(1)}, f32[2,256]{1,0:T(2,128)S(1)}, u32[]{:S(2)}, u32[]{:S(2)}) collective-permute-start(f32[2,256]{1,0:T(2,128)S(1)} %get-tuple-element.118), channel_id=1, source_target_pairs={{8,0},{16,8},{24,16},{9,1},{17,9},{25,17},{10,2},{18,10},{26,18},{... | collective-permute-start | bytes 6152 | tf_op jit(solution)/shard_map/ppermute | solution.py:15
  296.6 120.0 %reduce-scatter.31.cloned.1.call-start = ((), (), s32[]{:S(2)}) async-start(), calls=%async_computation.11 | async-start | bytes 1179648
  315.8 145.7 %collective-permute-start.27 = (f32[2,40,512]{2,1,0:T(8,128)}, f32[2,40,512]{2,1,0:T(8,128)}, u32[]{:S(2)}, u32[]{:S(2)}) collective-permute-start(f32[2,40,512]{2,1,0:T(8,128)} %get-tuple-element.68), channel_id=1, source_target_pairs={{0,8},{8,16},{16,24},{1,9},{9,17},{17,25},{2,10},{10,18},{18,26},{... | collective-permute-start | bytes 491528 | tf_op jit(solution)/shard_map/ppermute | solution.py:15
  319.2 144.1 %collective-permute-start.26 = (f32[2,40,512]{2,1,0:T(8,128)}, f32[2,40,512]{2,1,0:T(8,128)}, u32[]{:S(2)}, u32[]{:S(2)}) collective-permute-start(f32[2,40,512]{2,1,0:T(8,128)} %get-tuple-element.67), channel_id=1, source_target_pairs={{8,0},{16,8},{24,16},{9,1},{17,9},{25,17},{10,2},{18,10},{26,18},{... | collective-permute-start | bytes 491528 | tf_op jit(solution)/shard_map/ppermute | solution.py:15
  322.3 143.5 %collective-permute-start.24 = (f32[2,160,1]{2,1,0:T(8,128)}, f32[2,160,1]{2,1,0:T(8,128)}, u32[]{:S(2)}, u32[]{:S(2)}) collective-permute-start(f32[2,160,1]{2,1,0:T(8,128)} %get-tuple-element.63), channel_id=1, source_target_pairs={{0,1},{1,2},{2,3},{3,4},{4,5},{5,6},{6,7},{8,9},{9,10},{10,11},{11... | collective-permute-start | bytes 3848 | tf_op jit(solution)/shard_map/ppermute | solution.py:31
  324.2 141.6 %collective-permute-start.25 = (f32[2,160,1]{2,1,0:T(8,128)}, f32[2,160,1]{2,1,0:T(8,128)}, u32[]{:S(2)}, u32[]{:S(2)}) collective-permute-start(f32[2,160,1]{2,1,0:T(8,128)} %get-tuple-element.64), channel_id=1, source_target_pairs={{1,0},{2,1},{3,2},{4,3},{5,4},{6,5},{7,6},{9,8},{10,9},{11,10},{12... | collective-permute-start | bytes 3848 | tf_op jit(solution)/shard_map/ppermute | solution.py:33
  346.3 17.3 %collective-permute-start.17 = (f32[2,256]{1,0:T(2,128)S(1)}, f32[2,256]{1,0:T(2,128)S(1)}, u32[]{:S(2)}, u32[]{:S(2)}) collective-permute-start(f32[2,256]{1,0:T(2,128)S(1)} %get-tuple-element.115), channel_id=1, source_target_pairs={{0,8},{8,16},{16,24},{1,9},{9,17},{17,25},{2,10},{10,18},{18,26},{... | collective-permute-start | bytes 6152 | tf_op jit(solution)/shard_map/ppermute | solution.py:15
  363.6 17.0 %collective-permute-start.16 = (f32[2,256]{1,0:T(2,128)S(1)}, f32[2,256]{1,0:T(2,128)S(1)}, u32[]{:S(2)}, u32[]{:S(2)}) collective-permute-start(f32[2,256]{1,0:T(2,128)S(1)} %get-tuple-element.114), channel_id=1, source_target_pairs={{8,0},{16,8},{24,16},{9,1},{17,9},{25,17},{10,2},{18,10},{26,18},{... | collective-permute-start | bytes 6152 | tf_op jit(solution)/shard_map/ppermute | solution.py:15
  375.9 53.8 %copy-start.52 = (f32[2,4,256]{2,1,0:T(4,128)S(1)}, f32[2,4,256]{2,1,0:T(4,128)}, u32[]{:S(2)}) copy-start(f32[2,4,256]{2,1,0:T(4,128)} %param.10) | copy-start | bytes 24580
  380.5 121.3 %reduce-scatter.33.cloned.1.call-start = ((), (), s32[]{:S(2)}) async-start(), calls=%async_computation.12 | async-start | bytes 1179648
  430.4 5.5 collective-permute-start.23
  435.8 9.0 %collective-permute-start.22 = (f32[2,256]{1,0:T(2,128)}, f32[2,256]{1,0:T(2,128)S(1)}, u32[]{:S(2)}, u32[]{:S(2)}) collective-permute-start(f32[2,256]{1,0:T(2,128)} %get-tuple-element.110), channel_id=1, source_target_pairs={{8,0},{16,8},{24,16},{9,1},{17,9},{25,17},{10,2},{18,10},{26,18},{... | collective-permute-start | bytes 6152 | tf_op jit(solution)/shard_map/ppermute | solution.py:15
  453.1 133.5 %reduce-scatter.35.cloned.1.call-start = ((), (), s32[]{:S(2)}) async-start(), calls=%async_computation.13 | async-start | bytes 1179648
  488.4 57.9 %collective-permute-start.33 = (f32[2,40,512]{2,1,0:T(8,128)}, f32[2,40,512]{2,1,0:T(8,128)}, u32[]{:S(2)}, u32[]{:S(2)}) collective-permute-start(f32[2,40,512]{2,1,0:T(8,128)} %get-tuple-element.59), channel_id=1, source_target_pairs={{0,8},{8,16},{16,24},{1,9},{9,17},{17,25},{2,10},{10,18},{18,26},{... | collective-permute-start | bytes 491528 | tf_op jit(solution)/shard_map/ppermute | solution.py:15
  492.2 55.9 %collective-permute-start.32 = (f32[2,40,512]{2,1,0:T(8,128)}, f32[2,40,512]{2,1,0:T(8,128)}, u32[]{:S(2)}, u32[]{:S(2)}) collective-permute-start(f32[2,40,512]{2,1,0:T(8,128)} %get-tuple-element.58), channel_id=1, source_target_pairs={{8,0},{16,8},{24,16},{9,1},{17,9},{25,17},{10,2},{18,10},{26,18},{... | collective-permute-start | bytes 491528 | tf_op jit(solution)/shard_map/ppermute | solution.py:15
  494.9 55.7 %collective-permute-start.30 = (f32[2,160,1]{2,1,0:T(8,128)}, f32[2,160,1]{2,1,0:T(8,128)}, u32[]{:S(2)}, u32[]{:S(2)}) collective-permute-start(f32[2,160,1]{2,1,0:T(8,128)} %get-tuple-element.54), channel_id=1, source_target_pairs={{0,1},{1,2},{2,3},{3,4},{4,5},{5,6},{6,7},{8,9},{9,10},{10,11},{11... | collective-permute-start | bytes 3848 | tf_op jit(solution)/shard_map/ppermute | solution.py:31
  496.8 53.8 %collective-permute-start.31 = (f32[2,160,1]{2,1,0:T(8,128)}, f32[2,160,1]{2,1,0:T(8,128)}, u32[]{:S(2)}, u32[]{:S(2)}) collective-permute-start(f32[2,160,1]{2,1,0:T(8,128)} %get-tuple-element.55), channel_id=1, source_target_pairs={{1,0},{2,1},{3,2},{4,3},{5,4},{6,5},{7,6},{9,8},{10,9},{11,10},{12... | collective-permute-start | bytes 3848 | tf_op jit(solution)/shard_map/ppermute | solution.py:33
  516.1 5.5 collective-permute-start.29
  521.5 16.6 %collective-permute-start.28 = (f32[2,256]{1,0:T(2,128)}, f32[2,256]{1,0:T(2,128)}, u32[]{:S(2)}, u32[]{:S(2)}) collective-permute-start(f32[2,256]{1,0:T(2,128)} %get-tuple-element.106), channel_id=1, source_target_pairs={{8,0},{16,8},{24,16},{9,1},{17,9},{25,17},{10,2},{18,10},{26,18},{... | collective-permute-start | bytes 6152 | tf_op jit(solution)/shard_map/ppermute | solution.py:15
  538.0 52.5 %copy-start.55 = (f32[4,256]{1,0:T(4,128)S(1)}, f32[4,256]{1,0:T(4,128)}, u32[]{:S(2)}) copy-start(f32[4,256]{1,0:T(4,128)} %copy-done.54) | copy-start | bytes 12292
  538.1 122.0 %reduce-scatter.37.cloned.1.call-start = ((), (), s32[]{:S(2)}) async-start(), calls=%async_computation.14 | async-start | bytes 1179648
  573.7 90.2 %collective-permute-start.39 = (f32[2,40,512]{2,1,0:T(8,128)}, f32[2,40,512]{2,1,0:T(8,128)}, u32[]{:S(2)}, u32[]{:S(2)}) collective-permute-start(f32[2,40,512]{2,1,0:T(8,128)} %get-tuple-element.50), channel_id=1, source_target_pairs={{0,8},{8,16},{16,24},{1,9},{9,17},{17,25},{2,10},{10,18},{18,26},{... | collective-permute-start | bytes 491528 | tf_op jit(solution)/shard_map/ppermute | solution.py:15
  577.5 88.1 %collective-permute-start.38 = (f32[2,40,512]{2,1,0:T(8,128)}, f32[2,40,512]{2,1,0:T(8,128)}, u32[]{:S(2)}, u32[]{:S(2)}) collective-permute-start(f32[2,40,512]{2,1,0:T(8,128)} %get-tuple-element.49), channel_id=1, source_target_pairs={{8,0},{16,8},{24,16},{9,1},{17,9},{25,17},{10,2},{18,10},{26,18},{... | collective-permute-start | bytes 491528 | tf_op jit(solution)/shard_map/ppermute | solution.py:15
  580.2 88.0 %collective-permute-start.36 = (f32[2,160,1]{2,1,0:T(8,128)}, f32[2,160,1]{2,1,0:T(8,128)}, u32[]{:S(2)}, u32[]{:S(2)}) collective-permute-start(f32[2,160,1]{2,1,0:T(8,128)} %get-tuple-element.45), channel_id=1, source_target_pairs={{0,1},{1,2},{2,3},{3,4},{4,5},{5,6},{6,7},{8,9},{9,10},{10,11},{11... | collective-permute-start | bytes 3848 | tf_op jit(solution)/shard_map/ppermute | solution.py:31
  582.1 86.0 %collective-permute-start.37 = (f32[2,160,1]{2,1,0:T(8,128)}, f32[2,160,1]{2,1,0:T(8,128)}, u32[]{:S(2)}, u32[]{:S(2)}) collective-permute-start(f32[2,160,1]{2,1,0:T(8,128)} %get-tuple-element.46), channel_id=1, source_target_pairs={{1,0},{2,1},{3,2},{4,3},{5,4},{6,5},{7,6},{9,8},{10,9},{11,10},{12... | collective-permute-start | bytes 3848 | tf_op jit(solution)/shard_map/ppermute | solution.py:33
  601.0 5.5 collective-permute-start.35
  606.4 16.5 %collective-permute-start.34 = (f32[2,256]{1,0:T(2,128)}, f32[2,256]{1,0:T(2,128)}, u32[]{:S(2)}, u32[]{:S(2)}) collective-permute-start(f32[2,256]{1,0:T(2,128)} %get-tuple-element.102), channel_id=1, source_target_pairs={{8,0},{16,8},{24,16},{9,1},{17,9},{25,17},{10,2},{18,10},{26,18},{... | collective-permute-start | bytes 6152 | tf_op jit(solution)/shard_map/ppermute | solution.py:15
  622.9 149.5 %reduce-scatter.39.cloned.1.call-start = ((), (), s32[]{:S(2)}) async-start(), calls=%async_computation.15 | async-start | bytes 1179648
  701.8 17.3 %collective-permute-start.41 = (f32[2,256]{1,0:T(2,128)S(1)}, f32[2,256]{1,0:T(2,128)S(1)}, u32[]{:S(2)}, u32[]{:S(2)}) collective-permute-start(f32[2,256]{1,0:T(2,128)S(1)} %get-tuple-element.99), channel_id=1, source_target_pairs={{0,8},{8,16},{16,24},{1,9},{9,17},{17,25},{2,10},{10,18},{18,26},{... | collective-permute-start | bytes 6152 | tf_op jit(solution)/shard_map/ppermute | solution.py:15
  706.0 67.8 %collective-permute-start.45 = (f32[2,40,512]{2,1,0:T(8,128)}, f32[2,40,512]{2,1,0:T(8,128)}, u32[]{:S(2)}, u32[]{:S(2)}) collective-permute-start(f32[2,40,512]{2,1,0:T(8,128)} %get-tuple-element.41), channel_id=1, source_target_pairs={{0,8},{8,16},{16,24},{1,9},{9,17},{17,25},{2,10},{10,18},{18,26},{... | collective-permute-start | bytes 491528 | tf_op jit(solution)/shard_map/ppermute | solution.py:15
  709.4 66.2 %collective-permute-start.44 = (f32[2,40,512]{2,1,0:T(8,128)}, f32[2,40,512]{2,1,0:T(8,128)}, u32[]{:S(2)}, u32[]{:S(2)}) collective-permute-start(f32[2,40,512]{2,1,0:T(8,128)} %get-tuple-element.40), channel_id=1, source_target_pairs={{8,0},{16,8},{24,16},{9,1},{17,9},{25,17},{10,2},{18,10},{26,18},{... | collective-permute-start | bytes 491528 | tf_op jit(solution)/shard_map/ppermute | solution.py:15
  712.5 65.6 %collective-permute-start.42 = (f32[2,160,1]{2,1,0:T(8,128)}, f32[2,160,1]{2,1,0:T(8,128)}, u32[]{:S(2)}, u32[]{:S(2)}) collective-permute-start(f32[2,160,1]{2,1,0:T(8,128)} %get-tuple-element.36), channel_id=1, source_target_pairs={{0,1},{1,2},{2,3},{3,4},{4,5},{5,6},{6,7},{8,9},{9,10},{10,11},{11... | collective-permute-start | bytes 3848 | tf_op jit(solution)/shard_map/ppermute | solution.py:31
  714.4 63.6 %collective-permute-start.43 = (f32[2,160,1]{2,1,0:T(8,128)}, f32[2,160,1]{2,1,0:T(8,128)}, u32[]{:S(2)}, u32[]{:S(2)}) collective-permute-start(f32[2,160,1]{2,1,0:T(8,128)} %get-tuple-element.37), channel_id=1, source_target_pairs={{1,0},{2,1},{3,2},{4,3},{5,4},{6,5},{7,6},{9,8},{10,9},{11,10},{12... | collective-permute-start | bytes 3848 | tf_op jit(solution)/shard_map/ppermute | solution.py:33
  719.1 16.8 %collective-permute-start.40 = (f32[2,256]{1,0:T(2,128)}, f32[2,256]{1,0:T(2,128)}, u32[]{:S(2)}, u32[]{:S(2)}) collective-permute-start(f32[2,256]{1,0:T(2,128)} %get-tuple-element.98), channel_id=1, source_target_pairs={{8,0},{16,8},{24,16},{9,1},{17,9},{25,17},{10,2},{18,10},{26,18},{... | collective-permute-start | bytes 6152 | tf_op jit(solution)/shard_map/ppermute | solution.py:15
  728.1 50.0 %copy-start.64 = (f32[160]{0:T(256)S(1)}, f32[160]{0:T(256)}, u32[]{:S(2)}) copy-start(f32[160]{0:T(256)} %get-tuple-element.133) | copy-start | bytes 1924
  728.1 50.0 %copy-start.70 = (f32[2,160]{1,0:T(2,128)S(1)}, f32[2,160]{1,0:T(2,128)}, u32[]{:S(2)}) copy-start(f32[2,160]{1,0:T(2,128)} %get-tuple-element.10) | copy-start | bytes 3844
  781.7 38.5 %collective-permute-start.49 = (f32[2,40,512]{2,1,0:T(8,128)}, f32[2,40,512]{2,1,0:T(8,128)}, u32[]{:S(2)}, u32[]{:S(2)}) collective-permute-start(f32[2,40,512]{2,1,0:T(8,128)} %get-tuple-element.29), channel_id=1, source_target_pairs={{0,8},{8,16},{16,24},{1,9},{9,17},{17,25},{2,10},{10,18},{18,26},{... | collective-permute-start | bytes 491528 | tf_op jit(solution)/shard_map/ppermute | solution.py:15
  785.1 36.7 %collective-permute-start.48 = (f32[2,40,512]{2,1,0:T(8,128)}, f32[2,40,512]{2,1,0:T(8,128)}, u32[]{:S(2)}, u32[]{:S(2)}) collective-permute-start(f32[2,40,512]{2,1,0:T(8,128)} %get-tuple-element.28), channel_id=1, source_target_pairs={{8,0},{16,8},{24,16},{9,1},{17,9},{25,17},{10,2},{18,10},{26,18},{... | collective-permute-start | bytes 491528 | tf_op jit(solution)/shard_map/ppermute | solution.py:15
  789.1 35.0 %collective-permute-start.46 = (f32[2,160,1]{2,1,0:T(8,128)}, f32[2,160,1]{2,1,0:T(8,128)}, u32[]{:S(2)}, u32[]{:S(2)}) collective-permute-start(f32[2,160,1]{2,1,0:T(8,128)} %get-tuple-element.30), channel_id=1, source_target_pairs={{0,1},{1,2},{2,3},{3,4},{4,5},{5,6},{6,7},{8,9},{9,10},{10,11},{11... | collective-permute-start | bytes 3848 | tf_op jit(solution)/shard_map/ppermute | solution.py:31
  791.1 33.1 %collective-permute-start.47 = (f32[2,160,1]{2,1,0:T(8,128)}, f32[2,160,1]{2,1,0:T(8,128)}, u32[]{:S(2)}, u32[]{:S(2)}) collective-permute-start(f32[2,160,1]{2,1,0:T(8,128)} %get-tuple-element.32), channel_id=1, source_target_pairs={{1,0},{2,1},{3,2},{4,3},{5,4},{6,5},{7,6},{9,8},{10,9},{11,10},{12... | collective-permute-start | bytes 3848 | tf_op jit(solution)/shard_map/ppermute | solution.py:33
  (68 other events, 1206.1 us)
Sparse Core Ops, SparseCore 0:
  113.8 34.1 reduce-scatter.24
  213.6 35.9 reduce-scatter.26
  296.7 36.1 reduce-scatter.28
  380.6 35.9 reduce-scatter.30
  453.3 36.6 reduce-scatter.32
  538.2 36.7 reduce-scatter.34
  623.1 36.9 reduce-scatter.36
  736.0 36.3 reduce-scatter.38
where the time goes:
time: 847 us; the launch traced here: 835 us
  matrix products  174 us (21%)
  blocking collectives  169 us (20%)
  starting transfers between devices  156 us (18%)
  waiting for transfers between devices  152 us (18%)
  local copies, waits for them, and re-layouts  136 us (16%)
  other arithmetic  31.5 us (4%)
  between operations  17 us (2%)
    unnamed x16, waiting for transfers between devices  148 us
    ppermute x34, starting transfers between devices, from_behind(): return lax.ppermute(block, axis, route)  103 us
    unnamed x181, local copies, waits for them, and re-layouts  95.9 us
    psum x7, blocking collectives, reduce_partials(): boundary = lax.psum(partial_boundary, 'outer')  92.6 us
    dot_general x8, matrix products, local(): jnp.einsum('lij,plj->pli', dipole, gathered[:, 1:], precision=highest)  79.2 us
    all_gather x8, blocking collectives, local(): gathered = lax.all_gather(extended, 'outer', axis=2, tiled=True)  63.2 us
    dot_general x8, matrix products, local(): jnp.einsum('lji,plj->pli', source_blocks, source_rows, precision=highest)  55.2 us
    ppermute x8, starting transfers between devices, with_halo(): lax.ppermute(head, axis, [((i + 1) % count, i) for i in range(ends)])  36.4 us
  transfers between devices with their start and end apart: 58, of which 9 were waited for; matrix products, arithmetic and copies ran while one was open for 36% of the time, Pallas kernels for 0%

commit v1 on v0

--- a/solution.py
+++ b/solution.py
@@ -7,6 +7,10 @@
 ORDER = 4
 kinetic_scale = 3.125
 time_step = 0.1
+
+
+def fields_touch(patch):
+    return jnp.sum(lax.all_gather(patch, "outer"), axis=0)
 
 
 def from_behind(block, axis, distance):
@@ -39,7 +43,7 @@
 
 def reduce_partials(partial_terms, partial_boundary):
     own_terms = lax.psum_scatter(partial_terms, "outer", scatter_dimension=2, tiled=True)
-    boundary = lax.psum(partial_boundary, "outer")
+    boundary = fields_touch(partial_boundary)
     return (own_terms, boundary)
 
 

time: 847 us -> 892 us (1.053)
  blocking collectives: 169 us -> 189 us
  waiting for transfers between devices: 152 us -> 164 us
    psum x7 -> x0, blocking collectives: 92.6 us -> none  [reduce_partials(): boundary = lax.psum(partial_boundary, 'outer')]
    all_gather x0 -> x8, blocking collectives: none -> 65.1 us  [fields_touch(): return jnp.sum(lax.all_gather(patch, 'outer'), axis=0)]
    psum x1 -> x4, blocking collectives: 13.1 us -> 54.3 us  [spread(): return lax.psum(jnp.where(mine, shard, jnp.zeros_like(shard)), axis)]
    ppermute x34, waiting for transfers between devices: 3.96 us -> 14.9 us  [from_behind(): return lax.ppermute(block, axis, route)]
    unnamed x181 -> x161, local copies, waits for them, and re-layouts: 95.9 us -> 95.7 us
  transfers between devices with their start and end apart: 58 -> 58, of which waited for: 9 -> 9; matrix products, arithmetic and copies ran while one was open for 36% -> 34% of each run, Pallas kernels for 0% -> 0%
where the time goes in v1:
time: 892 us; the launch traced here: 881 us
  blocking collectives  189 us (21%)
  matrix products  177 us (20%)
  waiting for transfers between devices  164 us (18%)
  starting transfers between devices  154 us (17%)
  local copies, waits for them, and re-layouts  144 us (16%)
  other arithmetic  36 us (4%)
  between operations  16.5 us (2%)
    unnamed x16, waiting for transfers between devices  149 us
    ppermute x34, starting transfers between devices, from_behind(): return lax.ppermute(block, axis, route)  105 us
    unnamed x161, local copies, waits for them, and re-layouts  95.7 us
    dot_general x8, matrix products, local(): jnp.einsum('lij,plj->pli', dipole, gathered[:, 1:], precision=highest)  79.6 us
    all_gather x8, blocking collectives, local(): gathered = lax.all_gather(extended, 'outer', axis=2, tiled=True)  69.5 us
    all_gather x8, blocking collectives, fields_touch(): return jnp.sum(lax.all_gather(patch, 'outer'), axis=0)  65.1 us
    dot_general x8, matrix products, local(): jnp.einsum('lji,plj->pli', source_blocks, source_rows, precision=highest)  55.2 us
    psum x4, blocking collectives, spread(): return lax.psum(jnp.where(mine, shard, jnp.zeros_like(shard)), axis)  54.3 us
  transfers between devices with their start and end apart: 58, of which 9 were waited for; matrix products, arithmetic and copies ran while one was open for 34% of the time, Pallas kernels for 0%

profile of v1, /device:TPU:12, one launch (start us, length us, event | category | flops | bytes accessed | tf_op | source)
XLA Modules:
  0.0 881.0 jit_solution(4318822683819910728)
XLA Ops:
  37.8 6.2 slice.446
  44.0 9.1 %all-gather = f32[16,4,40]{2,1,0:T(4,128)S(1)} all-gather(f32[2,4,40]{2,1,0:T(4,128)S(1)} %copy.114), channel_id=2, replica_groups=mesh['inner'=4,'outer'=8] {'outer'}, dimensions={0}, use_global_device_ids=true | all-gather | bytes 11520 | tf_op jit(solution)/shard_map/all_gather | solution.py:13
  57.3 8.1 all_gather.72
  65.4 3.8 collective-permute-start.1
  84.8 4.6 collective-permute-start.14
  91.3 14.7 %all-reduce.3 = (f32[2,4,40]{2,0,1:T(2,128)S(1)}, f32[2,4,40]{2,0,1:T(2,128)S(1)}) all-reduce(f32[2,4,40]{2,0,1:T(2,128)S(1)} %copy.113, f32[2,4,40]{2,0,1:T(2,128)S(1)} %copy.125), channel_id=1, replica_groups=mesh['inner'=4,'outer'=8] {'outer'}, use_global_device_ids=true, to_apply=%region_1.2 | all-reduce | flops 640 | bytes 5120 | tf_op jit(solution)/shard_map/psum | solution.py:24
  108.4 14.2 %collective-permute-done.15 = f32[2,40,512]{2,1,0:T(8,128)} collective-permute-done((f32[2,40,512]{2,1,0:T(8,128)}, f32[2,40,512]{2,1,0:T(8,128)}, u32[]{:S(2)}, u32[]{:S(2)}) %collective-permute-start.15) | collective-permute-done | bytes 163872 | tf_op jit(solution)/shard_map/ppermute | solution.py:19
  127.7 7.4 convolution_bitcast_fusion.7
  135.2 4.2 copy.197
  139.4 4.5 reshape.181
  147.7 32.4 %reduce-scatter.25.cloned.1.call-done = f32[256,8]{1,0:T(8,128)} async-done(((f32[2048,8]{1,0:T(8,128)}), f32[256,8]{1,0:T(8,128)}) %reduce-scatter.25.cloned.1.call-update) | async-done | bytes 8208
  183.3 9.9 %fusion.55 = f32[2,4,256]{2,0,1:T(2,128)S(1)} fusion(f32[2,4,256]{2,0,1:T(2,128)S(1)} %fusion.63, f32[2,4,256]{2,0,1:T(2,128)S(1)} %copy.198, f32[2,5,2048]{2,0,1:T(2,128)S(1)} %all_gather.72, f32[4,256,2048]{2,1,0:T(8,128)} %param.13, f32[2,4,256]{2,0,1:T(2,128)S(1)} %copy-done.44, f32[]{:T(128)} %bitcast, f32[4,256]{1,0:T(4,128)S(1)} %copy-done.46, ...), kind=kOutput, calls=%fused_computation.81 | convolution fusion | flops 50343936 | bytes 8511492 | tf_op jit(solution)/shard_map/lij,plj->pli/dot_general | solution.py:89
  193.5 8.2 all-gather.1
  212.0 3.6 collective-permute-start.21
  222.1 4.5 collective-permute-start.19
  226.6 6.8 convolution_bitcast_fusion.6
  236.6 4.5 reshape.183
  241.2 8.0 all_gather.73
  249.2 26.6 %reduce-scatter.27.cloned.1.call-done = f32[256,8]{1,0:T(8,128)} async-done(((f32[2048,8]{1,0:T(8,128)}), f32[256,8]{1,0:T(8,128)}) %reduce-scatter.27.cloned.1.call-update) | async-done | bytes 8208
  279.0 9.9 %fusion.50 = f32[2,4,256]{2,0,1:T(2,128)S(1)} fusion(f32[2,4,256]{2,0,1:T(2,128)S(1)} %fusion.62, f32[2,4,256]{2,0,1:T(2,128)S(1)} %copy.200, f32[2,5,2048]{2,0,1:T(2,128)S(1)} %all_gather.73, f32[4,256,2048]{2,1,0:T(8,128)} %param.13, f32[4,256]{1,0:T(4,128)S(1)} %get-tuple-element.123, f32[]{:T(128)} %bitcast, f32[4,256]{1,0:T(4,128)S(1)} %compare_convert_fusion, ...), kind=kOutput, calls=%fused_computation.75 | convolution fusion | flops 50345984 | bytes 8511492 | tf_op jit(solution)/shard_map/lij,plj->pli/dot_general | solution.py:89
  292.6 8.2 all-gather.2
  304.2 6.8 convolution_bitcast_fusion.5
  314.2 4.5 reshape.185
  318.8 8.9 %all_gather.76 = f32[2,5,2048]{2,0,1:T(2,128)S(1)} all-gather(f32[2,5,256]{2,0,1:T(2,128)S(1)} %pad_maximum_fusion.25), channel_id=1, replica_groups=mesh['inner'=4,'outer'=8] {'outer'}, dimensions={2}, use_global_device_ids=true | all-gather | bytes 92160 | tf_op jit(solution)/shard_map/all_gather | solution.py:87
  337.9 13.8 %all-reduce.2 = (f32[2,4,40]{2,0,1:T(2,128)S(1)}, f32[2,4,40]{2,0,1:T(2,128)S(1)}) all-reduce(f32[2,4,40]{2,0,1:T(2,128)S(1)} %copy-done.54, f32[2,4,40]{2,0,1:T(2,128)S(1)} %copy.137), channel_id=1, replica_groups=mesh['inner'=4,'outer'=8] {'outer'}, use_global_device_ids=true, to_apply=%region_7.8 | all-reduce | flops 640 | bytes 5120 | tf_op jit(solution)/shard_map/psum | solution.py:24
  361.1 4.9 collective-permute-start.25
  369.3 9.9 %fusion.45 = f32[2,4,256]{2,0,1:T(2,128)S(1)} fusion(f32[2,4,256]{2,0,1:T(2,128)S(1)} %fusion.61, f32[2,4,256]{2,0,1:T(2,128)S(1)} %copy.202, f32[2,5,2048]{2,0,1:T(2,128)S(1)} %all_gather.76, f32[4,256,2048]{2,1,0:T(8,128)} %param.13, f32[4,256]{1,0:T(4,128)S(1)} %get-tuple-element.124, f32[]{:T(128)} %bitcast, f32[4,256]{1,0:T(4,128)S(1)} %compare_convert_fusion, ...), kind=kOutput, calls=%fused_computation.69 | convolution fusion | flops 50345984 | bytes 8511492 | tf_op jit(solution)/shard_map/lij,plj->pli/dot_general | solution.py:89
  382.3 7.0 all-gather.3
  393.1 6.8 convolution_bitcast_fusion.4
  403.1 4.6 reshape.187
  407.7 10.2 %all_gather.79 = f32[2,5,2048]{2,0,1:T(2,128)S(1)} all-gather(f32[2,5,256]{2,0,1:T(2,128)S(1)} %pad_maximum_fusion.26), channel_id=1, replica_groups=mesh['inner'=4,'outer'=8] {'outer'}, dimensions={2}, use_global_device_ids=true | all-gather | bytes 92160 | tf_op jit(solution)/shard_map/all_gather | solution.py:87
  418.0 27.8 %reduce-scatter.31.cloned.1.call-done = f32[256,8]{1,0:T(8,128)} async-done(((f32[2048,8]{1,0:T(8,128)}), f32[256,8]{1,0:T(8,128)}) %reduce-scatter.31.cloned.1.call-update) | async-done | bytes 8208
  449.0 9.9 %fusion.40 = f32[2,4,256]{2,0,1:T(2,128)S(1)} fusion(f32[2,4,256]{2,0,1:T(2,128)} %fusion.60, f32[2,4,256]{2,0,1:T(2,128)S(1)} %copy.204, f32[2,5,2048]{2,0,1:T(2,128)S(1)} %all_gather.79, f32[4,256,2048]{2,1,0:T(8,128)} %param.13, f32[4,256]{1,0:T(4,128)S(1)} %get-tuple-element.122, f32[]{:T(128)} %bitcast, f32[4,256]{1,0:T(4,128)S(1)} %compare_convert_fusion, ...), kind=kOutput, calls=%fused_computation.63 | convolution fusion | flops 50345984 | bytes 8511492 | tf_op jit(solution)/shard_map/lij,plj->pli/dot_general | solution.py:89
  463.2 8.2 all-gather.4
  474.6 6.8 convolution_bitcast_fusion.3
  485.1 4.5 reshape.189
  489.8 9.2 %all_gather.82 = f32[2,5,2048]{2,0,1:T(2,128)S(1)} all-gather(f32[2,5,256]{2,0,1:T(2,128)} %pad_maximum_fusion.27), channel_id=1, replica_groups=mesh['inner'=4,'outer'=8] {'outer'}, dimensions={2}, use_global_device_ids=true | all-gather | bytes 92160 | tf_op jit(solution)/shard_map/all_gather | solution.py:87
  517.3 4.5 collective-permute-start.31
  523.2 4.1 reduce-scatter.33.cloned.1.call-done
  542.7 12.7 %all-reduce.1 = (f32[2,4,40]{2,0,1:T(2,128)}, f32[2,4,40]{2,0,1:T(2,128)}) all-reduce(f32[2,4,40]{2,0,1:T(2,128)S(1)} %copy.143, f32[2,4,40]{2,0,1:T(2,128)} %copy.153), channel_id=1, replica_groups=mesh['inner'=4,'outer'=8] {'outer'}, use_global_device_ids=true, to_apply=%region_13.14 | all-reduce | flops 640 | bytes 5120 | tf_op jit(solution)/shard_map/psum | solution.py:24
  556.4 9.9 %fusion.35 = f32[2,4,256]{2,0,1:T(2,128)S(1)} fusion(f32[2,4,256]{2,0,1:T(2,128)S(1)} %fusion.59, f32[2,4,256]{2,0,1:T(2,128)} %copy.206, f32[2,5,2048]{2,0,1:T(2,128)S(1)} %all_gather.82, f32[4,256,2048]{2,1,0:T(8,128)} %param.13, f32[2,4,256]{2,0,1:T(2,128)S(1)} %fusion.196, f32[]{:T(128)} %bitcast.68, f32[4,256]{1,0:T(4,128)S(1)} %copy-done.46, ...), kind=kOutput, calls=%fused_computation.57 | convolution fusion | flops 50343936 | bytes 8511492 | tf_op jit(solution)/shard_map/lij,plj->pli/dot_general | solution.py:89
  575.7 8.2 all-gather.5
  584.5 4.4 collective-permute-start.39
  593.0 4.9 collective-permute-start.37
  598.0 6.8 convolution_bitcast_fusion.2
  607.9 4.5 reshape.191
  613.2 8.0 all_gather.85
  621.2 26.9 %reduce-scatter.35.cloned.1.call-done = f32[256,8]{1,0:T(8,128)} async-done(((f32[2048,8]{1,0:T(8,128)}), f32[256,8]{1,0:T(8,128)}) %reduce-scatter.35.cloned.1.call-update) | async-done | bytes 8208
  651.9 9.9 %fusion.30 = f32[2,4,256]{2,0,1:T(2,128)S(1)} fusion(f32[2,4,256]{2,0,1:T(2,128)} %fusion.58, f32[2,4,256]{2,0,1:T(2,128)} %copy.208, f32[2,5,2048]{2,0,1:T(2,128)S(1)} %all_gather.85, f32[4,256,2048]{2,1,0:T(8,128)} %param.13, f32[]{:T(128)} %bitcast.68, f32[4,256]{1,0:T(4,128)S(1)} %copy-done.48, f32[4,256]{1,0:T(4,128)S(1)} %compare_convert_fusion, ...), kind=kOutput, calls=%fused_computation.51 | convolution fusion | flops 50345984 | bytes 8511492 | tf_op jit(solution)/shard_map/lij,plj->pli/dot_general | solution.py:89
  666.1 8.2 all-gather.6
  677.6 6.8 convolution_bitcast_fusion.1
  688.1 4.5 reshape.193
  692.7 8.9 %all_gather.88 = f32[2,5,2048]{2,0,1:T(2,128)S(1)} all-gather(f32[2,5,256]{2,0,1:T(2,128)} %pad_maximum_fusion.29), channel_id=1, replica_groups=mesh['inner'=4,'outer'=8] {'outer'}, dimensions={2}, use_global_device_ids=true | all-gather | bytes 92160 | tf_op jit(solution)/shard_map/all_gather | solution.py:87
  720.1 4.5 collective-permute-start.43
  747.5 13.0 %all-reduce = (f32[2,4,40]{2,0,1:T(2,128)}, f32[2,4,40]{2,0,1:T(2,128)}) all-reduce(f32[2,4,40]{2,0,1:T(2,128)} %copy.165, f32[2,4,40]{2,0,1:T(2,128)} %copy.159), channel_id=1, replica_groups=mesh['inner'=4,'outer'=8] {'outer'}, use_global_device_ids=true, to_apply=%region_22.23 | all-reduce | flops 640 | bytes 5120 | tf_op jit(solution)/shard_map/psum | solution.py:24
  761.4 9.9 %fusion.25 = f32[2,4,256]{2,0,1:T(2,128)S(1)} fusion(f32[2,4,256]{2,0,1:T(2,128)S(1)} %fusion.57, f32[2,4,256]{2,0,1:T(2,128)} %copy.210, f32[2,5,2048]{2,0,1:T(2,128)S(1)} %all_gather.88, f32[4,256,2048]{2,1,0:T(8,128)} %param.13, f32[]{:T(128)} %bitcast.68, f32[4,256]{1,0:T(4,128)S(1)} %get-tuple-element.124, f32[4,256]{1,0:T(4,128)S(1)} %compare_convert_fusion, ...), kind=kOutput, calls=%fused_computation.45 | convolution fusion | flops 50345984 | bytes 8511492 | tf_op jit(solution)/shard_map/lij,plj->pli/dot_general | solution.py:89
  772.7 8.1 all-gather.7
  781.0 4.0 collective-permute-start.49
  789.4 4.5 collective-permute-start.47
  801.3 6.8 convolution_bitcast_fusion
  811.3 4.5 reshape.195
  816.6 8.3 all_gather.91
  824.8 28.2 %reduce-scatter.39.cloned.1.call-done = f32[256,8]{1,0:T(8,128)} async-done(((f32[2048,8]{1,0:T(8,128)}), f32[256,8]{1,0:T(8,128)}) %reduce-scatter.39.cloned.1.call-update) | async-done | bytes 8208
  854.6 10.4 %fusion.20 = f32[2,4,256]{2,0,1:T(2,128)S(1)} fusion(f32[2,4,256]{2,0,1:T(2,128)S(1)} %copy-done.53, f32[2,4,256]{2,0,1:T(2,128)S(1)} %copy.212, f32[2,5,2048]{2,0,1:T(2,128)S(1)} %all_gather.91, f32[4,256,2048]{2,1,0:T(8,128)} %param.13, f32[]{:T(128)} %bitcast.68, f32[4,256]{1,0:T(4,128)S(1)} %get-tuple-element.122, ...), kind=kOutput, calls=%fused_computation.39 | convolution fusion | flops 50345984 | bytes 8511492 | tf_op jit(solution)/shard_map/lij,plj->pli/dot_general | solution.py:89
  (444 shorter events, 285.3 us)
Async XLA Ops:
  7.2 172.9 %reduce-scatter.25.cloned.1.call-start = ((), (), s32[]{:S(2)}) async-start(), calls=%async_computation.8 | async-start | bytes 1179648
  9.2 56.2 %collective-permute-start.9 = (f32[40,40]{0,1:T(8,128)S(1)}, f32[40,40]{0,1:T(8,128)S(1)}, u32[]{:S(2)}, u32[]{:S(2)}) collective-permute-start(f32[40,40]{0,1:T(8,128)S(1)} %slice_bitcast_fusion.17), channel_id=1, source_target_pairs={{0,8},{8,16},{16,24},{1,9},{9,17},{17,25},{2,10},{10,18},{18,26},{... | collective-permute-start | bytes 19208 | tf_op jit(solution)/shard_map/ppermute | solution.py:19
  14.4 54.8 %collective-permute-start.8 = (f32[2,40,512]{2,1,0:T(8,128)S(1)}, f32[2,40,512]{2,1,0:T(8,128)}, u32[]{:S(2)}, u32[]{:S(2)}) collective-permute-start(f32[2,40,512]{2,1,0:T(8,128)S(1)} %get-tuple-element.89), channel_id=1, source_target_pairs={{0,8},{8,16},{16,24},{1,9},{9,17},{17,25},{2,10},{10,18},{18,26},{... | collective-permute-start | bytes 491528 | tf_op jit(solution)/shard_map/ppermute | solution.py:19
  17.9 56.0 %collective-permute-start.7 = (f32[2,40,512]{2,1,0:T(8,128)}, f32[2,40,512]{2,1,0:T(8,128)S(1)}, u32[]{:S(2)}, u32[]{:S(2)}) collective-permute-start(f32[2,40,512]{2,1,0:T(8,128)} %get-tuple-element.88), channel_id=1, source_target_pairs={{8,0},{16,8},{24,16},{9,1},{17,9},{25,17},{10,2},{18,10},{26,18},{... | collective-permute-start | bytes 491528 | tf_op jit(solution)/shard_map/ppermute | solution.py:19
  22.7 53.6 %collective-permute-start.5 = (f32[2,160,1]{2,1,0:T(8,128)}, f32[2,160,1]{2,1,0:T(8,128)S(1)}, u32[]{:S(2)}, u32[]{:S(2)}) collective-permute-start(f32[2,160,1]{2,1,0:T(8,128)} %get-tuple-element.78), channel_id=1, source_target_pairs={{0,1},{1,2},{2,3},{3,4},{4,5},{5,6},{6,7},{8,9},{9,10},{10,11},{11... | collective-permute-start | bytes 3848 | tf_op jit(solution)/shard_map/ppermute | solution.py:35
  26.7 27.2 %collective-permute-start = (f32[2,256]{1,0:T(2,128)S(1)}, f32[2,256]{1,0:T(2,128)S(1)}, u32[]{:S(2)}, u32[]{:S(2)}) collective-permute-start(f32[2,256]{1,0:T(2,128)S(1)} %get-tuple-element.120), channel_id=1, source_target_pairs={{8,0},{16,8},{24,16},{9,1},{17,9},{25,17},{10,2},{18,10},{26,18},{... | collective-permute-start | bytes 6152 | tf_op jit(solution)/shard_map/ppermute | solution.py:19
  36.5 242.6 %copy-start.47 = (f32[4,256]{1,0:T(4,128)}, f32[4,256]{1,0:T(4,128)S(1)}, u32[]{:S(2)}) copy-start(f32[4,256]{1,0:T(4,128)S(1)} %get-tuple-element.123) | copy-start | bytes 12292
  53.9 22.4 %collective-permute-start.6 = (f32[2,160,1]{2,1,0:T(8,128)}, f32[2,160,1]{2,1,0:T(8,128)S(1)}, u32[]{:S(2)}, u32[]{:S(2)}) collective-permute-start(f32[2,160,1]{2,1,0:T(8,128)} %get-tuple-element.79), channel_id=1, source_target_pairs={{1,0},{2,1},{3,2},{4,3},{5,4},{6,5},{7,6},{9,8},{10,9},{11,10},{12... | collective-permute-start | bytes 3848 | tf_op jit(solution)/shard_map/ppermute | solution.py:37
  57.3 70.4 %slice-start = ((f32[2,4,256]{2,0,1:T(2,128)}), f32[2,3,256]{2,0,1:T(2,128)S(1)}, s32[]{:S(2)}) async-start(f32[2,4,256]{2,0,1:T(2,128)} %copy-done.43), calls=%async_computation.16 | async-start | bytes 12288 | tf_op jit(solution)/shard_map/slice | solution.py:96
  65.4 62.3 %collective-permute-start.1 = (f32[2,256]{1,0:T(2,128)}, f32[2,256]{1,0:T(2,128)S(1)}, u32[]{:S(2)}, u32[]{:S(2)}) collective-permute-start(f32[2,256]{1,0:T(2,128)} %get-tuple-element.121), channel_id=1, source_target_pairs={{0,8},{8,16},{16,24},{1,9},{9,17},{17,25},{2,10},{10,18},{18,26},{... | collective-permute-start | bytes 6152 | tf_op jit(solution)/shard_map/ppermute | solution.py:19
  69.2 58.5 %collective-permute-start.2 = (f32[256,2048]{1,0:T(8,128)}, f32[256,2048]{1,0:T(8,128)S(1)}, u32[]{:S(2)}, u32[]{:S(2)}) collective-permute-start(f32[256,2048]{1,0:T(8,128)} %slice_bitcast_fusion), channel_id=1, source_target_pairs={{0,8},{8,16},{16,24},{1,9},{9,17},{17,25},{2,10},{10,18},{18,26},{... | collective-permute-start | bytes 6291464 | tf_op jit(solution)/shard_map/ppermute | solution.py:19
  82.8 39.7 %collective-permute-start.15 = (f32[2,40,512]{2,1,0:T(8,128)}, f32[2,40,512]{2,1,0:T(8,128)}, u32[]{:S(2)}, u32[]{:S(2)}) collective-permute-start(f32[2,40,512]{2,1,0:T(8,128)} %get-tuple-element.83), channel_id=1, source_target_pairs={{0,8},{8,16},{16,24},{1,9},{9,17},{17,25},{2,10},{10,18},{18,26},{... | collective-permute-start | bytes 491528 | tf_op jit(solution)/shard_map/ppermute | solution.py:19
  84.8 59.3 %collective-permute-start.14 = (f32[2,40,512]{2,1,0:T(8,128)}, f32[2,40,512]{2,1,0:T(8,128)}, u32[]{:S(2)}, u32[]{:S(2)}) collective-permute-start(f32[2,40,512]{2,1,0:T(8,128)} %get-tuple-element.82), channel_id=1, source_target_pairs={{8,0},{16,8},{24,16},{9,1},{17,9},{25,17},{10,2},{18,10},{26,18},{... | collective-permute-start | bytes 491528 | tf_op jit(solution)/shard_map/ppermute | solution.py:19
  89.4 112.4 %collective-permute-start.12 = (f32[2,160,1]{2,1,0:T(8,128)}, f32[2,160,1]{2,1,0:T(8,128)}, u32[]{:S(2)}, u32[]{:S(2)}) collective-permute-start(f32[2,160,1]{2,1,0:T(8,128)} %get-tuple-element.75), channel_id=1, source_target_pairs={{0,1},{1,2},{2,3},{3,4},{4,5},{5,6},{6,7},{8,9},{9,10},{10,11},{11... | collective-permute-start | bytes 3848 | tf_op jit(solution)/shard_map/ppermute | solution.py:35
  122.6 79.2 %collective-permute-start.13 = (f32[2,160,1]{2,1,0:T(8,128)}, f32[2,160,1]{2,1,0:T(8,128)}, u32[]{:S(2)}, u32[]{:S(2)}) collective-permute-start(f32[2,160,1]{2,1,0:T(8,128)} %get-tuple-element.76), channel_id=1, source_target_pairs={{1,0},{2,1},{3,2},{4,3},{5,4},{6,5},{7,6},{9,8},{10,9},{11,10},{12... | collective-permute-start | bytes 3848 | tf_op jit(solution)/shard_map/ppermute | solution.py:37
  144.0 131.8 %reduce-scatter.27.cloned.1.call-start = ((), (), s32[]{:S(2)}) async-start(), calls=%async_computation.9 | async-start | bytes 1179648
  206.2 35.0 %collective-permute-start.3 = (f32[2,256]{1,0:T(2,128)S(1)}, f32[2,256]{1,0:T(2,128)S(1)}, u32[]{:S(2)}, u32[]{:S(2)}) collective-permute-start(f32[2,256]{1,0:T(2,128)S(1)} %get-tuple-element.116), channel_id=1, source_target_pairs={{8,0},{16,8},{24,16},{9,1},{17,9},{25,17},{10,2},{18,10},{26,18},{... | collective-permute-start | bytes 6152 | tf_op jit(solution)/shard_map/ppermute | solution.py:19
  208.6 13.5 %collective-permute-start.4 = (f32[2,256]{1,0:T(2,128)S(1)}, f32[2,256]{1,0:T(2,128)S(1)}, u32[]{:S(2)}, u32[]{:S(2)}) collective-permute-start(f32[2,256]{1,0:T(2,128)S(1)} %get-tuple-element.117), channel_id=1, source_target_pairs={{0,8},{8,16},{16,24},{1,9},{9,17},{17,25},{2,10},{10,18},{18,26},{... | collective-permute-start | bytes 6152 | tf_op jit(solution)/shard_map/ppermute | solution.py:19
  212.0 115.7 %collective-permute-start.21 = (f32[2,40,512]{2,1,0:T(8,128)}, f32[2,40,512]{2,1,0:T(8,128)}, u32[]{:S(2)}, u32[]{:S(2)}) collective-permute-start(f32[2,40,512]{2,1,0:T(8,128)} %get-tuple-element.71), channel_id=1, source_target_pairs={{0,8},{8,16},{16,24},{1,9},{9,17},{17,25},{2,10},{10,18},{18,26},{... | collective-permute-start | bytes 491528 | tf_op jit(solution)/shard_map/ppermute | solution.py:19
  215.6 113.9 %collective-permute-start.20 = (f32[2,40,512]{2,1,0:T(8,128)}, f32[2,40,512]{2,1,0:T(8,128)}, u32[]{:S(2)}, u32[]{:S(2)}) collective-permute-start(f32[2,40,512]{2,1,0:T(8,128)} %get-tuple-element.70), channel_id=1, source_target_pairs={{8,0},{16,8},{24,16},{9,1},{17,9},{25,17},{10,2},{18,10},{26,18},{... | collective-permute-start | bytes 491528 | tf_op jit(solution)/shard_map/ppermute | solution.py:19
  219.5 112.6 %collective-permute-start.18 = (f32[2,160,1]{2,1,0:T(8,128)}, f32[2,160,1]{2,1,0:T(8,128)}, u32[]{:S(2)}, u32[]{:S(2)}) collective-permute-start(f32[2,160,1]{2,1,0:T(8,128)} %get-tuple-element.60), channel_id=1, source_target_pairs={{0,1},{1,2},{2,3},{3,4},{4,5},{5,6},{6,7},{8,9},{9,10},{10,11},{11... | collective-permute-start | bytes 3848 | tf_op jit(solution)/shard_map/ppermute | solution.py:35
  222.1 110.0 %collective-permute-start.19 = (f32[2,160,1]{2,1,0:T(8,128)}, f32[2,160,1]{2,1,0:T(8,128)}, u32[]{:S(2)}, u32[]{:S(2)}) collective-permute-start(f32[2,160,1]{2,1,0:T(8,128)} %get-tuple-element.61), channel_id=1, source_target_pairs={{1,0},{2,1},{3,2},{4,3},{5,4},{6,5},{7,6},{9,8},{10,9},{11,10},{12... | collective-permute-start | bytes 3848 | tf_op jit(solution)/shard_map/ppermute | solution.py:37
  241.1 125.0 %reduce-scatter.29.cloned.1.call-start = ((), (), s32[]{:S(2)}) async-start(), calls=%async_computation.10 | async-start | bytes 1179648
  289.2 12.3 %collective-permute-start.11 = (f32[2,256]{1,0:T(2,128)S(1)}, f32[2,256]{1,0:T(2,128)S(1)}, u32[]{:S(2)}, u32[]{:S(2)}) collective-permute-start(f32[2,256]{1,0:T(2,128)S(1)} %get-tuple-element.113), channel_id=1, source_target_pairs={{0,8},{8,16},{16,24},{1,9},{9,17},{17,25},{2,10},{10,18},{18,26},{... | collective-permute-start | bytes 6152 | tf_op jit(solution)/shard_map/ppermute | solution.py:19
  301.5 9.5 %collective-permute-start.10 = (f32[2,256]{1,0:T(2,128)S(1)}, f32[2,256]{1,0:T(2,128)S(1)}, u32[]{:S(2)}, u32[]{:S(2)}) collective-permute-start(f32[2,256]{1,0:T(2,128)S(1)} %get-tuple-element.112), channel_id=1, source_target_pairs={{8,0},{16,8},{24,16},{9,1},{17,9},{25,17},{10,2},{18,10},{26,18},{... | collective-permute-start | bytes 6152 | tf_op jit(solution)/shard_map/ppermute | solution.py:19
  318.7 127.1 %reduce-scatter.31.cloned.1.call-start = ((), (), s32[]{:S(2)}) async-start(), calls=%async_computation.11 | async-start | bytes 1179648
  352.7 146.3 %collective-permute-start.27 = (f32[2,40,512]{2,1,0:T(8,128)}, f32[2,40,512]{2,1,0:T(8,128)}, u32[]{:S(2)}, u32[]{:S(2)}) collective-permute-start(f32[2,40,512]{2,1,0:T(8,128)} %get-tuple-element.65), channel_id=1, source_target_pairs={{0,8},{8,16},{16,24},{1,9},{9,17},{17,25},{2,10},{10,18},{18,26},{... | collective-permute-start | bytes 491528 | tf_op jit(solution)/shard_map/ppermute | solution.py:19
  356.1 144.7 %collective-permute-start.26 = (f32[2,40,512]{2,1,0:T(8,128)}, f32[2,40,512]{2,1,0:T(8,128)}, u32[]{:S(2)}, u32[]{:S(2)}) collective-permute-start(f32[2,40,512]{2,1,0:T(8,128)} %get-tuple-element.64), channel_id=1, source_target_pairs={{8,0},{16,8},{24,16},{9,1},{17,9},{25,17},{10,2},{18,10},{26,18},{... | collective-permute-start | bytes 491528 | tf_op jit(solution)/shard_map/ppermute | solution.py:19
  359.2 144.2 %collective-permute-start.24 = (f32[2,160,1]{2,1,0:T(8,128)}, f32[2,160,1]{2,1,0:T(8,128)}, u32[]{:S(2)}, u32[]{:S(2)}) collective-permute-start(f32[2,160,1]{2,1,0:T(8,128)} %get-tuple-element.57), channel_id=1, source_target_pairs={{0,1},{1,2},{2,3},{3,4},{4,5},{5,6},{6,7},{8,9},{9,10},{10,11},{11... | collective-permute-start | bytes 3848 | tf_op jit(solution)/shard_map/ppermute | solution.py:35
  361.1 142.3 %collective-permute-start.25 = (f32[2,160,1]{2,1,0:T(8,128)}, f32[2,160,1]{2,1,0:T(8,128)}, u32[]{:S(2)}, u32[]{:S(2)}) collective-permute-start(f32[2,160,1]{2,1,0:T(8,128)} %get-tuple-element.58), channel_id=1, source_target_pairs={{1,0},{2,1},{3,2},{4,3},{5,4},{6,5},{7,6},{9,8},{10,9},{11,10},{12... | collective-permute-start | bytes 3848 | tf_op jit(solution)/shard_map/ppermute | solution.py:37
  379.5 10.5 %collective-permute-start.17 = (f32[2,256]{1,0:T(2,128)S(1)}, f32[2,256]{1,0:T(2,128)S(1)}, u32[]{:S(2)}, u32[]{:S(2)}) collective-permute-start(f32[2,256]{1,0:T(2,128)S(1)} %get-tuple-element.109), channel_id=1, source_target_pairs={{0,8},{8,16},{16,24},{1,9},{9,17},{17,25},{2,10},{10,18},{18,26},{... | collective-permute-start | bytes 6152 | tf_op jit(solution)/shard_map/ppermute | solution.py:19
  390.1 17.7 %collective-permute-start.16 = (f32[2,256]{1,0:T(2,128)S(1)}, f32[2,256]{1,0:T(2,128)S(1)}, u32[]{:S(2)}, u32[]{:S(2)}) collective-permute-start(f32[2,256]{1,0:T(2,128)S(1)} %get-tuple-element.108), channel_id=1, source_target_pairs={{8,0},{16,8},{24,16},{9,1},{17,9},{25,17},{10,2},{18,10},{26,18},{... | collective-permute-start | bytes 6152 | tf_op jit(solution)/shard_map/ppermute | solution.py:19
  403.1 55.9 %copy-start.45 = (f32[2,4,256]{2,1,0:T(4,128)S(1)}, f32[2,4,256]{2,1,0:T(4,128)}, u32[]{:S(2)}) copy-start(f32[2,4,256]{2,1,0:T(4,128)} %param.10) | copy-start | bytes 24580
  407.7 119.6 %reduce-scatter.33.cloned.1.call-start = ((), (), s32[]{:S(2)}) async-start(), calls=%async_computation.12 | async-start | bytes 1179648
  459.8 12.3 %collective-permute-start.23 = (f32[2,256]{1,0:T(2,128)S(1)}, f32[2,256]{1,0:T(2,128)S(1)}, u32[]{:S(2)}, u32[]{:S(2)}) collective-permute-start(f32[2,256]{1,0:T(2,128)S(1)} %get-tuple-element.105), channel_id=1, source_target_pairs={{0,8},{8,16},{16,24},{1,9},{9,17},{17,25},{2,10},{10,18},{18,26},{... | collective-permute-start | bytes 6152 | tf_op jit(solution)/shard_map/ppermute | solution.py:19
  472.1 9.3 %collective-permute-start.22 = (f32[2,256]{1,0:T(2,128)}, f32[2,256]{1,0:T(2,128)S(1)}, u32[]{:S(2)}, u32[]{:S(2)}) collective-permute-start(f32[2,256]{1,0:T(2,128)} %get-tuple-element.104), channel_id=1, source_target_pairs={{8,0},{16,8},{24,16},{9,1},{17,9},{25,17},{10,2},{18,10},{26,18},{... | collective-permute-start | bytes 6152 | tf_op jit(solution)/shard_map/ppermute | solution.py:19
  489.7 158.4 %reduce-scatter.35.cloned.1.call-start = ((), (), s32[]{:S(2)}) async-start(), calls=%async_computation.13 | async-start | bytes 1179648
  508.0 23.1 %collective-permute-start.33 = (f32[2,40,512]{2,1,0:T(8,128)}, f32[2,40,512]{2,1,0:T(8,128)}, u32[]{:S(2)}, u32[]{:S(2)}) collective-permute-start(f32[2,40,512]{2,1,0:T(8,128)} %get-tuple-element.53), channel_id=1, source_target_pairs={{0,8},{8,16},{16,24},{1,9},{9,17},{17,25},{2,10},{10,18},{18,26},{... | collective-permute-start | bytes 491528 | tf_op jit(solution)/shard_map/ppermute | solution.py:19
  512.2 20.7 %collective-permute-start.32 = (f32[2,40,512]{2,1,0:T(8,128)}, f32[2,40,512]{2,1,0:T(8,128)}, u32[]{:S(2)}, u32[]{:S(2)}) collective-permute-start(f32[2,40,512]{2,1,0:T(8,128)} %get-tuple-element.52), channel_id=1, source_target_pairs={{8,0},{16,8},{24,16},{9,1},{17,9},{25,17},{10,2},{18,10},{26,18},{... | collective-permute-start | bytes 491528 | tf_op jit(solution)/shard_map/ppermute | solution.py:19
  515.3 20.2 %collective-permute-start.30 = (f32[2,160,1]{2,1,0:T(8,128)}, f32[2,160,1]{2,1,0:T(8,128)}, u32[]{:S(2)}, u32[]{:S(2)}) collective-permute-start(f32[2,160,1]{2,1,0:T(8,128)} %get-tuple-element.42), channel_id=1, source_target_pairs={{0,1},{1,2},{2,3},{3,4},{4,5},{5,6},{6,7},{8,9},{9,10},{10,11},{11... | collective-permute-start | bytes 3848 | tf_op jit(solution)/shard_map/ppermute | solution.py:35
  517.3 18.2 %collective-permute-start.31 = (f32[2,160,1]{2,1,0:T(8,128)}, f32[2,160,1]{2,1,0:T(8,128)}, u32[]{:S(2)}, u32[]{:S(2)}) collective-permute-start(f32[2,160,1]{2,1,0:T(8,128)} %get-tuple-element.43), channel_id=1, source_target_pairs={{1,0},{2,1},{3,2},{4,3},{5,4},{6,5},{7,6},{9,8},{10,9},{11,10},{12... | collective-permute-start | bytes 3848 | tf_op jit(solution)/shard_map/ppermute | solution.py:37
  569.0 43.5 %collective-permute-start.28 = (f32[2,256]{1,0:T(2,128)}, f32[2,256]{1,0:T(2,128)}, u32[]{:S(2)}, u32[]{:S(2)}) collective-permute-start(f32[2,256]{1,0:T(2,128)} %get-tuple-element.100), channel_id=1, source_target_pairs={{8,0},{16,8},{24,16},{9,1},{17,9},{25,17},{10,2},{18,10},{26,18},{... | collective-permute-start | bytes 6152 | tf_op jit(solution)/shard_map/ppermute | solution.py:19
  572.3 20.6 %collective-permute-start.29 = (f32[2,256]{1,0:T(2,128)S(1)}, f32[2,256]{1,0:T(2,128)S(1)}, u32[]{:S(2)}, u32[]{:S(2)}) collective-permute-start(f32[2,256]{1,0:T(2,128)S(1)} %get-tuple-element.101), channel_id=1, source_target_pairs={{0,8},{8,16},{16,24},{1,9},{9,17},{17,25},{2,10},{10,18},{18,26},{... | collective-permute-start | bytes 6152 | tf_op jit(solution)/shard_map/ppermute | solution.py:19
  584.5 117.1 %collective-permute-start.39 = (f32[2,40,512]{2,1,0:T(8,128)}, f32[2,40,512]{2,1,0:T(8,128)}, u32[]{:S(2)}, u32[]{:S(2)}) collective-permute-start(f32[2,40,512]{2,1,0:T(8,128)} %get-tuple-element.47), channel_id=1, source_target_pairs={{0,8},{8,16},{16,24},{1,9},{9,17},{17,25},{2,10},{10,18},{18,26},{... | collective-permute-start | bytes 491528 | tf_op jit(solution)/shard_map/ppermute | solution.py:19
  588.9 114.5 %collective-permute-start.38 = (f32[2,40,512]{2,1,0:T(8,128)}, f32[2,40,512]{2,1,0:T(8,128)}, u32[]{:S(2)}, u32[]{:S(2)}) collective-permute-start(f32[2,40,512]{2,1,0:T(8,128)} %get-tuple-element.46), channel_id=1, source_target_pairs={{8,0},{16,8},{24,16},{9,1},{17,9},{25,17},{10,2},{18,10},{26,18},{... | collective-permute-start | bytes 491528 | tf_op jit(solution)/shard_map/ppermute | solution.py:19
  591.0 115.0 %collective-permute-start.36 = (f32[2,160,1]{2,1,0:T(8,128)}, f32[2,160,1]{2,1,0:T(8,128)}, u32[]{:S(2)}, u32[]{:S(2)}) collective-permute-start(f32[2,160,1]{2,1,0:T(8,128)} %get-tuple-element.39), channel_id=1, source_target_pairs={{0,1},{1,2},{2,3},{3,4},{4,5},{5,6},{6,7},{8,9},{9,10},{10,11},{11... | collective-permute-start | bytes 3848 | tf_op jit(solution)/shard_map/ppermute | solution.py:35
  593.0 113.0 %collective-permute-start.37 = (f32[2,160,1]{2,1,0:T(8,128)}, f32[2,160,1]{2,1,0:T(8,128)}, u32[]{:S(2)}, u32[]{:S(2)}) collective-permute-start(f32[2,160,1]{2,1,0:T(8,128)} %get-tuple-element.40), channel_id=1, source_target_pairs={{1,0},{2,1},{3,2},{4,3},{5,4},{6,5},{7,6},{9,8},{10,9},{11,10},{12... | collective-permute-start | bytes 3848 | tf_op jit(solution)/shard_map/ppermute | solution.py:37
  597.9 54.0 %copy-start.48 = (f32[4,256]{1,0:T(4,128)S(1)}, f32[4,256]{1,0:T(4,128)}, u32[]{:S(2)}) copy-start(f32[4,256]{1,0:T(4,128)} %copy-done.47) | copy-start | bytes 12292
  612.5 117.8 %reduce-scatter.37.cloned.1.call-start = ((), (), s32[]{:S(2)}) async-start(), calls=%async_computation.14 | async-start | bytes 1179648
  662.7 12.3 %collective-permute-start.35 = (f32[2,256]{1,0:T(2,128)S(1)}, f32[2,256]{1,0:T(2,128)S(1)}, u32[]{:S(2)}, u32[]{:S(2)}) collective-permute-start(f32[2,256]{1,0:T(2,128)S(1)} %get-tuple-element.97), channel_id=1, source_target_pairs={{0,8},{8,16},{16,24},{1,9},{9,17},{17,25},{2,10},{10,18},{18,26},{... | collective-permute-start | bytes 6152 | tf_op jit(solution)/shard_map/ppermute | solution.py:19
  674.9 9.4 %collective-permute-start.34 = (f32[2,256]{1,0:T(2,128)}, f32[2,256]{1,0:T(2,128)S(1)}, u32[]{:S(2)}, u32[]{:S(2)}) collective-permute-start(f32[2,256]{1,0:T(2,128)} %get-tuple-element.96), channel_id=1, source_target_pairs={{8,0},{16,8},{24,16},{9,1},{17,9},{25,17},{10,2},{18,10},{26,18},{... | collective-permute-start | bytes 6152 | tf_op jit(solution)/shard_map/ppermute | solution.py:19
  692.7 160.4 %reduce-scatter.39.cloned.1.call-start = ((), (), s32[]{:S(2)}) async-start(), calls=%async_computation.15 | async-start | bytes 1179648
  710.3 23.8 %collective-permute-start.45 = (f32[2,40,512]{2,1,0:T(8,128)}, f32[2,40,512]{2,1,0:T(8,128)}, u32[]{:S(2)}, u32[]{:S(2)}) collective-permute-start(f32[2,40,512]{2,1,0:T(8,128)} %get-tuple-element.35), channel_id=1, source_target_pairs={{0,8},{8,16},{16,24},{1,9},{9,17},{17,25},{2,10},{10,18},{18,26},{... | collective-permute-start | bytes 491528 | tf_op jit(solution)/shard_map/ppermute | solution.py:19
  713.7 22.2 %collective-permute-start.44 = (f32[2,40,512]{2,1,0:T(8,128)}, f32[2,40,512]{2,1,0:T(8,128)}, u32[]{:S(2)}, u32[]{:S(2)}) collective-permute-start(f32[2,40,512]{2,1,0:T(8,128)} %get-tuple-element.34), channel_id=1, source_target_pairs={{8,0},{16,8},{24,16},{9,1},{17,9},{25,17},{10,2},{18,10},{26,18},{... | collective-permute-start | bytes 491528 | tf_op jit(solution)/shard_map/ppermute | solution.py:19
  718.2 20.3 %collective-permute-start.42 = (f32[2,160,1]{2,1,0:T(8,128)}, f32[2,160,1]{2,1,0:T(8,128)}, u32[]{:S(2)}, u32[]{:S(2)}) collective-permute-start(f32[2,160,1]{2,1,0:T(8,128)} %get-tuple-element.28), channel_id=1, source_target_pairs={{0,1},{1,2},{2,3},{3,4},{4,5},{5,6},{6,7},{8,9},{9,10},{10,11},{11... | collective-permute-start | bytes 3848 | tf_op jit(solution)/shard_map/ppermute | solution.py:35
  720.1 18.3 %collective-permute-start.43 = (f32[2,160,1]{2,1,0:T(8,128)}, f32[2,160,1]{2,1,0:T(8,128)}, u32[]{:S(2)}, u32[]{:S(2)}) collective-permute-start(f32[2,160,1]{2,1,0:T(8,128)} %get-tuple-element.29), channel_id=1, source_target_pairs={{1,0},{2,1},{3,2},{4,3},{5,4},{6,5},{7,6},{9,8},{10,9},{11,10},{12... | collective-permute-start | bytes 3848 | tf_op jit(solution)/shard_map/ppermute | solution.py:37
  781.0 84.7 %collective-permute-start.49 = (f32[2,40,512]{2,1,0:T(8,128)}, f32[2,40,512]{2,1,0:T(8,128)}, u32[]{:S(2)}, u32[]{:S(2)}) collective-permute-start(f32[2,40,512]{2,1,0:T(8,128)} %get-tuple-element.23), channel_id=1, source_target_pairs={{0,8},{8,16},{16,24},{1,9},{9,17},{17,25},{2,10},{10,18},{18,26},{... | collective-permute-start | bytes 491528 | tf_op jit(solution)/shard_map/ppermute | solution.py:19
  785.0 82.5 %collective-permute-start.48 = (f32[2,40,512]{2,1,0:T(8,128)}, f32[2,40,512]{2,1,0:T(8,128)}, u32[]{:S(2)}, u32[]{:S(2)}) collective-permute-start(f32[2,40,512]{2,1,0:T(8,128)} %get-tuple-element.22), channel_id=1, source_target_pairs={{8,0},{16,8},{24,16},{9,1},{17,9},{25,17},{10,2},{18,10},{26,18},{... | collective-permute-start | bytes 491528 | tf_op jit(solution)/shard_map/ppermute | solution.py:19
  787.5 82.5 %collective-permute-start.46 = (f32[2,160,1]{2,1,0:T(8,128)}, f32[2,160,1]{2,1,0:T(8,128)}, u32[]{:S(2)}, u32[]{:S(2)}) collective-permute-start(f32[2,160,1]{2,1,0:T(8,128)} %get-tuple-element.24), channel_id=1, source_target_pairs={{0,1},{1,2},{2,3},{3,4},{4,5},{5,6},{6,7},{8,9},{9,10},{10,11},{11... | collective-permute-start | bytes 3848 | tf_op jit(solution)/shard_map/ppermute | solution.py:35
  789.4 80.6 %collective-permute-start.47 = (f32[2,160,1]{2,1,0:T(8,128)}, f32[2,160,1]{2,1,0:T(8,128)}, u32[]{:S(2)}, u32[]{:S(2)}) collective-permute-start(f32[2,160,1]{2,1,0:T(8,128)} %get-tuple-element.26), channel_id=1, source_target_pairs={{1,0},{2,1},{3,2},{4,3},{5,4},{6,5},{7,6},{9,8},{10,9},{11,10},{12... | collective-permute-start | bytes 3848 | tf_op jit(solution)/shard_map/ppermute | solution.py:37
  793.9 5.5 collective-permute-start.41
  799.4 16.5 %collective-permute-start.40 = (f32[2,256]{1,0:T(2,128)}, f32[2,256]{1,0:T(2,128)}, u32[]{:S(2)}, u32[]{:S(2)}) collective-permute-start(f32[2,256]{1,0:T(2,128)} %get-tuple-element.92), channel_id=1, source_target_pairs={{8,0},{16,8},{24,16},{9,1},{17,9},{25,17},{10,2},{18,10},{26,18},{... | collective-permute-start | bytes 6152 | tf_op jit(solution)/shard_map/ppermute | solution.py:19
  811.3 53.7 %copy-start.52 = (f32[1,4,256]{2,0,1:T(1,128)S(1)}, f32[1,4,256]{2,0,1:T(1,128)}, u32[]{:S(2)}) copy-start(f32[1,4,256]{2,0,1:T(1,128)} %copy-done.51) | copy-start | bytes 12292
  815.9 54.2 %copy-start.56 = (f32[160]{0:T(256)S(1)}, f32[160]{0:T(256)}, u32[]{:S(2)}) copy-start(f32[160]{0:T(256)} %get-tuple-element.125) | copy-start | bytes 1924
  (58 other events, 849.6 us)
Sparse Core Ops, SparseCore 0:
  144.1 35.8 reduce-scatter.24
  241.3 34.4 reduce-scatter.26
  318.9 37.0 reduce-scatter.28
  407.8 37.9 reduce-scatter.30
  489.8 37.4 reduce-scatter.32
  612.6 35.4 reduce-scatter.34
  692.8 37.4 reduce-scatter.36
  816.0 37.0 reduce-scatter.38
